TPU v7x, 32 devices: a whole 2x2x4 slice. The times are simulated.
32 devices in a mesh: gx: 8 (over z, y), yz: 4 (over x, core).
Axes of the slice: x: 2, y: 2, z: 4, core: 2. Of those that a mesh axis runs over, the one named last changes fastest.
Arguments:
- solvent_vel: float32 [3, 256, 128, 2, 128], P(None, 'gx', 'yz'), may hold values from -6 to 6
- occupancy: int32 [256, 128, 128], P('gx', 'yz'), may hold values from 0 to 2
- grid_shift: int32 [3], replicated, may hold values from 1 to 3
- axis_index: int32 [64, 32, 64], P('gx', 'yz'), may hold values from 0 to 63
- colloid_pos: float32 [3, 8, 4, 128], P(None, 'gx', 'yz'), may hold values from 0 to 64, as said below
- colloid_vel: float32 [3, 8, 4, 128], P(None, 'gx', 'yz'), may hold values from -6 to 6
- colloid_mass: float32 [8, 4, 128], P('gx', 'yz'), may hold values from 2 to 20
- colloid_count: int32 [8, 4], P('gx', 'yz'), may hold values from 21 to 128, as said below
Outputs:
- solvent_out: float32 [3, 256, 128, 2, 128], P(None, 'gx', 'yz')
- colloid_pos_out: float32 [3, 8, 4, 128], P(None, 'gx', 'yz')
- colloid_vel_out: float32 [3, 8, 4, 128], P(None, 'gx', 'yz')
Inputs may be any that keep to these rules, and one draw needn't show every extreme that they name: `colloid_pos`: component 0 lies in [0, 8), component 1 in [0, 8), component 2 in [0, 64). `colloid_count`: some device holds 128 live colloids in every draw.
All inputs are finite; a program needn't handle non-finite values.
Results may differ from a plain program's by a relative error of at most 0.0003.
Values sent between devices are 32-bit elements; how exact they have to be, the bound alone decides.
A program may use at most 320 MiB of HBM per device.

v0:
```python
import functools
import math

import jax
import jax.numpy as jnp
from jax import lax
from jax.experimental import pallas as pl
from jax.experimental.pallas import tpu as pltpu
from jax.sharding import PartitionSpec as P

CX = 8
CY = 8
CZ = 64
SUB = 4
SUBSTEPS = 4
DIRECTIONS = 64


turn_angle = 130.0 * math.pi / 180.0
cos_angle = math.cos(turn_angle)
sin_angle = math.sin(turn_angle)
golden = math.pi * (3.0 - math.sqrt(5.0))
cutoff = 1.5
stiffness = 20.0
timestep = 0.05
fill_mass = 16.0
MESH = pl.DeviceIdType.MESH


def iota(shape, dim):
    return lax.broadcasted_iota(jnp.int32, shape, dim)


def three_terms(value):
    high = value.astype(jnp.bfloat16)
    rest = value - high.astype(jnp.float32)
    middle = rest.astype(jnp.bfloat16)
    low = (rest - middle.astype(jnp.float32)).astype(jnp.bfloat16)
    return (high, middle, low)


def dot(left, right, contract=((1,), (0,))):
    return lax.dot_general(left, right, (contract, ((), ())), preferred_element_type=jnp.float32)


def wrapped(value, size):
    return jnp.where(value >= size, value - size, value)


def layer_of(row, scale, width):
    return jnp.clip(jnp.floor(row * scale).astype(jnp.int32), 0, width - 1)


def accumulate(shape, steps, shift_x, solvent, occupancy, acc):
    width_x, width_y, width_z = shape
    block_x = width_x // steps
    rows = 2 * width_y
    step = pl.program_id(0)

    @pl.when(step == 0)
    def _():
        acc[...] = jnp.zeros_like(acc)

    double = (iota((rows, width_y), 0) >> 1 == iota((rows, width_y), 1)).astype(jnp.bfloat16)
    slot = (iota((rows, width_z), 0) & 1).astype(jnp.float32)
    for first in range(0, block_x, SUB):
        cell = step * (block_x // SUB) + first // SUB
        filled = [occupancy[first + r].astype(jnp.float32) for r in range(SUB)]
        live = [dot(double, f.astype(jnp.bfloat16)) > slot for f in filled]
        for c in range(4):
            size = rows if c < 3 else width_y
            at = pl.ds(c * rows, size)
            near = jnp.zeros((size, width_z), jnp.float32)
            far = near
            for r in range(SUB):
                value = jnp.where(live[r], solvent[c, first + r], 0.0) if c < 3 else filled[r]
                stays = jnp.broadcast_to(shift_x + r, (size, width_z)) < SUB
                near = near + jnp.where(stays, value, 0.0)
                far = far + jnp.where(stays, 0.0, value)
            acc[cell, at, :] += near
            acc[cell + 1, at, :] += far


def cell_sums(shape, shift, count, pos, vel, mass, part, acc):
    width_x, width_y, width_z = shape
    cells_x, cells_y = (width_x // SUB + 1, width_y // SUB + 1)
    rows = 2 * width_y
    shift_x, shift_y, shift_z = (shift[0], shift[1], shift[2])
    total = 3 * rows + width_y
    column = iota((cells_y * 8, total), 1)
    target = iota((cells_y * 8, total), 0)
    heavy = column >= 3 * rows
    which = jnp.where(heavy, 3, (column >= rows).astype(jnp.int32) + (column >= 2 * rows).astype(jnp.int32))
    layer = jnp.where(heavy, column - 3 * rows, (column - which * rows) >> 1)
    fits = jnp.logical_and(which == (target & 7), ((layer + shift_y) >> 2) == (target >> 3))
    select = fits.astype(jnp.float32).astype(jnp.bfloat16)

    cell_x = (layer_of(pos[0, 0], SUB, width_x) + shift_x) >> 2
    cell_y = (layer_of(pos[1, 0], SUB, width_y) + shift_y) >> 2
    cell_z = wrapped(layer_of(pos[2, 0], 2.0, width_z) + shift_z, width_z) >> 1
    slots = mass.shape[2]
    alive = (iota((1, slots), 1) < count[0, 0]).astype(jnp.float32)
    weight = mass[0] * alive
    comp = iota((8, slots), 0)
    values = jnp.where(
        comp == 0,
        vel[0, 0] * weight,
        jnp.where(
            comp == 1,
            vel[1, 0] * weight,
            jnp.where(comp == 2, vel[2, 0] * weight, jnp.where(comp == 3, weight, 0.0)),
        ),
    )
    place = jnp.broadcast_to(cell_x * cells_y + cell_y, (8, slots))
    near = (wrapped(iota((width_z, slots), 0) + shift_z, width_z) >> 1) == cell_z
    near = near.astype(jnp.float32).astype(jnp.bfloat16)
    even = ((iota((cells_y * 8, width_z), 1) + shift_z) & 1) == 0
    for i in range(cells_x):
        sums = sum(dot(select, term) for term in three_terms(acc[i])[::-1])
        partner = jnp.where(
            even, pltpu.roll(sums, width_z - 1, 1), pltpu.roll(sums, 1, 1)
        )
        number = iota((cells_y, 8, slots), 0) + i * cells_y
        spread = jnp.where(number == place[None], values[None], 0.0).reshape(cells_y * 8, slots)
        deposit = sum(dot(term, near, ((1,), (1,))) for term in three_terms(spread)[::-1])
        part[i] = (sums + partner + deposit).reshape(cells_y, 8, width_z)


def exchange_kernel(
    shape, steps, shift, count, solvent, occupancy, axis, pos, vel, mass, fields, pos_out, vel_out,
    acc, part, halo_x, halo_y, halo_c, edge_x, edge_y, edge_c, sent, got, own, force,
    halo_sem, edge_sem, sent_sem, got_sem,
):
    width_x, width_y, width_z = shape
    n_x, n_y = (width_x // SUB, width_y // SUB)
    slots = mass.shape[2]
    me_x, me_y = (lax.axis_index("gx"), lax.axis_index("yz"))
    size_x, size_y = (lax.axis_size("gx"), lax.axis_size("yz"))
    shift_x, shift_y, shift_z = (shift[0], shift[1], shift[2])

    def device(a, b):
        return (lax.rem(me_x + a + size_x, size_x), lax.rem(me_y + b + size_y, size_y))

    around = [(a, b) for a in (-1, 0, 1) for b in (-1, 0, 1) if (a, b) != (0, 0)]
    barrier = pltpu.get_barrier_semaphore()
    grid_step = pl.program_id(0)

    @pl.when(grid_step == 0)
    def _():
        for a, b in around:
            pl.semaphore_signal(barrier, inc=1, device_id=device(a, b), device_id_type=MESH)

    accumulate(shape, steps, shift_x, solvent, occupancy, acc)

    @pl.when(grid_step == steps - 1)
    def _():
        alive = (iota((1, slots), 1) < count[0, 0]).astype(jnp.float32)
        comp = iota((8, slots), 0)

        def stacked(rows):
            out = jnp.zeros((8, slots), jnp.float32)
            for c, row in enumerate(rows):
                out = jnp.where(comp == c, row, out)
            return out

        def columns(rows):
            block = jnp.concatenate([rows, jnp.zeros((slots - 8, slots), jnp.float32)], axis=0)
            return block.T

        start_rows = stacked([pos[0, 0], pos[1, 0], pos[2, 0], alive, mass[0]])
        sent[0] = start_rows
        pl.semaphore_wait(barrier, len(around))

        def remote(src, dst, send, receive, where):
            return pltpu.make_async_remote_copy(
                src_ref=src, dst_ref=dst, send_sem=send, recv_sem=receive,
                device_id=where, device_id_type=MESH,
            )

        def exchange(step):
            copies = []
            for k, (a, b) in enumerate(around):
                copies.append(
                    remote(
                        sent.at[step], got.at[step, 7 - k],
                        sent_sem.at[step, k], got_sem.at[step, 7 - k], device(a, b),
                    )
                )
            for copy in copies:
                copy.start()
            return copies

        copies = exchange(0)

        cell_sums(shape, shift, count, pos, vel, mass, part, acc)
        halo = [
            remote(part.at[n_x, pl.ds(0, n_y)], halo_x, halo_sem.at[0], halo_sem.at[3], device(1, 0)),
            remote(part.at[pl.ds(0, n_x), n_y], halo_y, halo_sem.at[1], halo_sem.at[4], device(0, 1)),
            remote(part.at[n_x, n_y], halo_c, halo_sem.at[2], halo_sem.at[5], device(1, 1)),
        ]
        for copy in halo:
            copy.start()

        state = columns(start_rows)
        place = [state[:, c : c + 1] for c in range(3)]
        mass_column = state[:, 4:5]

        index = axis[...].reshape(n_x * n_y, width_z // 2).astype(jnp.float32).astype(jnp.bfloat16)
        cell_z = wrapped(iota((width_z // 2, width_z), 1) + shift_z, width_z) >> 1
        expand = (cell_z == iota((width_z // 2, width_z), 0)).astype(jnp.float32).astype(jnp.bfloat16)
        number = dot(index, expand)
        height = 1.0 - (2.0 * number + 1.0) / DIRECTIONS
        radius = jnp.sqrt(1.0 - height * height)
        phase = number * golden
        normal = [radius * jnp.cos(phase), radius * jnp.sin(phase), height]
        sub = iota((n_x * n_y, 8, width_z), 1)
        spread = [jnp.broadcast_to(n[:, None, :], (n_x * n_y, 8, width_z)) for n in normal]
        directions = jnp.where(sub == 3, spread[0], jnp.where(sub == 4, spread[1], spread[2]))
        fields[pl.ds(0, n_x), pl.ds(0, n_y)] = directions.reshape(n_x, n_y, 8, width_z)

        for copy in halo:
            copy.wait()
        sub = iota((n_y, 8, width_z), 1)
        for i in range(n_x):
            total = part[i, pl.ds(0, n_y)]
            first = halo_y[i][None]
            if i == 0:
                total = total + halo_x[...]
                first = first + halo_c[...][None]
            total = jnp.concatenate([total[:1] + first, total[1:]], axis=0)
            mean = total / jnp.maximum(total[:, 3:4, :], fill_mass)
            fields[i, pl.ds(0, n_y)] = jnp.where(sub < 3, mean, fields[i, pl.ds(0, n_y)])
        edges = [
            remote(fields.at[0, pl.ds(0, n_y)], edge_x, edge_sem.at[0], edge_sem.at[3], device(-1, 0)),
            remote(fields.at[pl.ds(0, n_x), 0], edge_y, edge_sem.at[1], edge_sem.at[4], device(0, -1)),
            remote(fields.at[0, 0], edge_c, edge_sem.at[2], edge_sem.at[5], device(-1, -1)),
        ]
        for copy in edges:
            copy.start()

        groups = [
            [(pair, k) for k, pair in enumerate(around) if 0 in pair],
            [(pair, k) for k, pair in enumerate(around) if 0 not in pair],
        ]
        wide = 32 if slots % 32 == 0 else 8

        def forces(step, copies, place):
            for c in range(3):
                own[c] = jnp.broadcast_to(place[c], (slots, slots))

            for sources in [[((0, 0), None)]] + groups:
                for _, k in sources:
                    if k is not None:
                        copies[7 - k].wait_recv()

                def block(r, carry, sources=sources):
                    at = pl.ds(pl.multiple_of(r * wide, 8), wide)
                    own_x, own_y, own_z = (own[0, at, :], own[1, at, :], own[2, at, :])
                    total = None
                    for (a, b), k in sources:
                        def row(c):
                            if k is None:
                                return sent[step, pl.ds(c, 1), :]
                            return got[step, k, pl.ds(c, 1), :]

                        diff_x = own_x - (row(0) + float(a * CX))
                        diff_y = own_y - (row(1) + float(b * CY))
                        high = own_z - row(2)
                        high = jnp.where(
                            high > 0.5 * CZ, high - CZ, jnp.where(high < -0.5 * CZ, high + CZ, high)
                        )
                        radius_sq = diff_x * diff_x + diff_y * diff_y + high * high
                        reach = 1.0 - radius_sq * (1.0 / (cutoff * cutoff))
                        weight = jnp.where(radius_sq < cutoff * cutoff, reach * reach, 0.0) * row(3)
                        parts = [weight * diff_x, weight * diff_y, weight * high]
                        total = parts if total is None else [total[c] + parts[c] for c in range(3)]
                    for c in range(3):
                        if sources[0][1] is None:
                            force[c, at, :] = total[c]
                        else:
                            force[c, at, :] += total[c]
                    return carry

                lax.fori_loop(0, slots // wide, block, 0)
            for copy in copies:
                copy.wait_send()
            return [stiffness * jnp.sum(force[c], axis=1, keepdims=True) for c in range(3)]

        push = forces(0, copies, place)

        for copy in edges:
            copy.wait()
        fields[n_x, pl.ds(0, n_y)] = edge_x[...]
        fields[pl.ds(0, n_x), n_y] = edge_y[...]
        fields[n_x, n_y] = edge_c[...]

        layer_z = layer_of(pos[2, 0], 2.0, width_z)
        cell_x = (layer_of(pos[0, 0], SUB, width_x) + shift_x) >> 2
        cell_y = (layer_of(pos[1, 0], SUB, width_y) + shift_y) >> 2
        target = jnp.broadcast_to(cell_x * (n_y + 1) + cell_y, (8, slots))
        chosen = (iota((width_z, slots), 0) == layer_z).astype(jnp.float32).astype(jnp.bfloat16)
        picked = jnp.zeros((8, slots), jnp.float32)
        for i in range(n_x + 1):
            rows = fields[i].reshape((n_y + 1) * 8, width_z)
            at_z = sum(dot(term, chosen) for term in three_terms(rows)[::-1])
            number = iota((n_y + 1, 8, slots), 0) + i * (n_y + 1)
            at_z = at_z.reshape(n_y + 1, 8, slots)
            picked = picked + jnp.sum(jnp.where(number == target[None], at_z, 0.0), axis=0)
        mean = [picked[c : c + 1] for c in range(3)]
        n = [picked[c : c + 1] for c in range(3, 6)]
        rel = [vel[c, 0] - mean[c] for c in range(3)]
        cross = [n[1] * rel[2] - n[2] * rel[1], n[2] * rel[0] - n[0] * rel[2], n[0] * rel[1] - n[1] * rel[0]]
        along = n[0] * rel[0] + n[1] * rel[1] + n[2] * rel[2]
        turned = [
            mean[c] + cos_angle * rel[c] + sin_angle * cross[c] + (1.0 - cos_angle) * along * n[c]
            for c in range(3)
        ]
        state = columns(stacked([jnp.where(alive > 0, turned[c], vel[c, 0]) for c in range(3)]))
        speed = [state[:, c : c + 1] for c in range(3)]

        lane = iota((slots, slots), 1)
        for step in range(SUBSTEPS):
            speed = [speed[c] + timestep * push[c] / mass_column for c in range(3)]
            place = [place[c] + timestep * speed[c] for c in range(3)]
            block = jnp.zeros((slots, slots), jnp.float32)
            for c, column in enumerate(place):
                block = jnp.where(lane == c, column, block)
            if step == SUBSTEPS - 1:
                for c, column in enumerate(speed):
                    block = jnp.where(lane == 3 + c, column, block)
            flipped = block.T[:8]
            if step < SUBSTEPS - 1:
                sent[step + 1] = jnp.where(comp == 3, alive, flipped)
                copies = exchange(step + 1)
                push = forces(step + 1, copies, place)
        for c in range(3):
            pos_out[c, 0] = jnp.where(alive > 0, flipped[c : c + 1], pos[c, 0])
            vel_out[c, 0] = jnp.where(alive > 0, flipped[3 + c : 4 + c], vel[c, 0])


def rotate_kernel(shape, steps, shift, solvent, occupancy, fields, pos, vel, out, pos_out, vel_out):
    width_x, width_y, width_z = shape
    block_x = width_x // steps
    n_y = width_y // SUB
    rows = 2 * width_y
    step = pl.program_id(0)
    shift_x, shift_y = (shift[0], shift[1])
    double = (iota((rows, width_y), 0) >> 1 == iota((rows, width_y), 1)).astype(jnp.bfloat16)
    row = iota((8, width_z), 0)
    slot = (row & 1).astype(jnp.float32)
    later = ((row >> 1) + shift_y) >= SUB

    @pl.when(step == 0)
    def _():
        pos_out[...] = pos[...]
        vel_out[...] = vel[...]

    def layer(x, carry):
        held = dot(double, occupancy[x].astype(jnp.float32).astype(jnp.bfloat16))
        cell = (step * block_x + x + shift_x) >> 2
        for b in range(n_y):
            at = pl.ds(8 * b, 8)
            both = [
                jnp.where(
                    later, fields[cell, b + 1, pl.ds(c, 1), :], fields[cell, b, pl.ds(c, 1), :]
                )
                for c in range(6)
            ]
            mean, n = (both[:3], both[3:])
            old = [solvent[c, x, at, :] for c in range(3)]
            rel = [old[c] - mean[c] for c in range(3)]
            along = (1.0 - cos_angle) * (n[0] * rel[0] + n[1] * rel[1] + n[2] * rel[2])
            cross = [
                n[1] * rel[2] - n[2] * rel[1],
                n[2] * rel[0] - n[0] * rel[2],
                n[0] * rel[1] - n[1] * rel[0],
            ]
            live = held[8 * b : 8 * b + 8] > slot
            for c in range(3):
                new = mean[c] + cos_angle * rel[c] + sin_angle * cross[c] + along * n[c]
                out[c, x, at, :] = jnp.where(live, new, old[c])
        return carry

    for x in range(block_x):
        layer(x, 0)


def per_device(
    solvent_vel,
    occupancy,
    grid_shift,
    axis_index,
    colloid_pos,
    colloid_vel,
    colloid_mass,
    colloid_count,
):
    shape = occupancy.shape
    width_x, width_y, width_z = shape
    rows = 2 * width_y
    n_x, n_y = (width_x // SUB, width_y // SUB)
    slots = colloid_mass.shape[2]
    steps = 4
    block_x = width_x // steps
    solvent = solvent_vel.reshape(3, width_x, rows, width_z)
    smem = pl.BlockSpec(memory_space=pltpu.SMEM)
    vmem = pl.BlockSpec(memory_space=pltpu.VMEM)
    solvent_spec = pl.BlockSpec((3, block_x, rows, width_z), lambda i: (0, i, 0, 0))
    occupancy_spec = pl.BlockSpec((block_x, width_y, width_z), lambda i: (i, 0, 0))
    cells = (n_x + 1, n_y + 1, 8, width_z)
    f32 = jnp.float32

    fields, pos_out, vel_out = pl.pallas_call(
        functools.partial(exchange_kernel, shape, steps),
        grid=(steps,),
        out_shape=[
            jax.ShapeDtypeStruct(cells, f32),
            jax.ShapeDtypeStruct(colloid_pos.shape, f32),
            jax.ShapeDtypeStruct(colloid_vel.shape, f32),
        ],
        in_specs=[smem, smem, solvent_spec, occupancy_spec] + [vmem] * 4,
        out_specs=[vmem] * 3,
        scratch_shapes=[
            pltpu.VMEM((n_x + 1, 3 * rows + width_y, width_z), f32),
            pltpu.VMEM(cells, f32),
            pltpu.VMEM((n_y, 8, width_z), f32),
            pltpu.VMEM((n_x, 8, width_z), f32),
            pltpu.VMEM((8, width_z), f32),
            pltpu.VMEM((n_y, 8, width_z), f32),
            pltpu.VMEM((n_x, 8, width_z), f32),
            pltpu.VMEM((8, width_z), f32),
            pltpu.VMEM((SUBSTEPS, 8, slots), f32),
            pltpu.VMEM((SUBSTEPS, 8, 8, slots), f32),
            pltpu.VMEM((3, slots, slots), f32),
            pltpu.VMEM((3, slots, slots), f32),
            pltpu.SemaphoreType.DMA((6,)),
            pltpu.SemaphoreType.DMA((6,)),
            pltpu.SemaphoreType.DMA((SUBSTEPS, 8)),
            pltpu.SemaphoreType.DMA((SUBSTEPS, 8)),
        ],
        compiler_params=pltpu.CompilerParams(collective_id=0, has_side_effects=True),
        name="exchange",
    )(grid_shift, colloid_count, solvent, occupancy, axis_index, colloid_pos, colloid_vel, colloid_mass)

    turns = 2
    thin = width_x // turns
    solvent_spec = pl.BlockSpec((3, thin, rows, width_z), lambda i: (0, i, 0, 0))
    occupancy_spec = pl.BlockSpec((thin, width_y, width_z), lambda i: (i, 0, 0))
    solvent_out, pos_out, vel_out = pl.pallas_call(
        functools.partial(rotate_kernel, shape, turns),
        out_shape=[
            jax.ShapeDtypeStruct(solvent.shape, f32),
            jax.ShapeDtypeStruct(colloid_pos.shape, f32),
            jax.ShapeDtypeStruct(colloid_vel.shape, f32),
        ],
        grid=(turns,),
        in_specs=[smem, solvent_spec, occupancy_spec, vmem, vmem, vmem],
        out_specs=[solvent_spec, vmem, vmem],
        name="rotate",
    )(grid_shift, solvent, occupancy, fields, pos_out, vel_out)
    return (solvent_out.reshape(solvent_vel.shape), pos_out, vel_out)


def solution(mesh):
    return jax.shard_map(
        per_device,
        mesh=mesh,
        in_specs=(
            P(None, "gx", "yz", None, None),
            P("gx", "yz", None),
            P(),
            P("gx", "yz", None),
            P(None, "gx", "yz", None),
            P(None, "gx", "yz", None),
            P("gx", "yz", None),
            P("gx", "yz"),
        ),
        out_specs=(
            P(None, "gx", "yz", None, None),
            P(None, "gx", "yz", None),
            P(None, "gx", "yz", None),
        ),
        check_vma=False,
    )
```

profile of v0, /device:TPU:0, one launch (start us, length us, event | category | flops | bytes accessed | tf_op | source)
XLA Modules:
  0.0 39.9 jit_solution(18408012260057470067)
XLA Ops:
  1.3 34.1 %exchange.1 = (f32[9,9,8,128]{3,2,1,0:T(8,128)}, f32[3,1,1,128]{3,2,1,0:T(1,128)}, f32[3,1,1,128]{3,2,1,0:T(1,128)}) custom-call(s32[3]{0:T(128)} %shift.3, s32[1,1]{1,0:T(1,128)S(6)} %copy.11.count, f32[3,32,64,128]{3,2,1,0:T(8,128)} %bitcast.2, s32[32,32,128]{2,1,0:T(8,128)} %occupancy.3, s32[8,8,64]{2,1,0:T(8,128)} %axis.1, f32[3,1,1,128]{3,2,1,0:T(1,128)} %pos.1, ...), custom_call_target="tpu_custom_call" | custom-call | tf_op jit(solution)/shard_map/exchange/pallas_call | solution.py:413
  35.3 4.6 %rotate.1 = (f32[3,32,64,128]{3,2,1,0:T(8,128)}, f32[3,1,1,128]{3,2,1,0:T(1,128)}, f32[3,1,1,128]{3,2,1,0:T(1,128)}) custom-call(s32[3]{0:T(128)} %shift.3, f32[3,32,64,128]{3,2,1,0:T(8,128)} %bitcast.3, s32[32,32,128]{2,1,0:T(8,128)} %occupancy.3, f32[9,9,8,128]{3,2,1,0:T(8,128)} %get-tuple-element.9.fields, f32[3,1,1,128]{3,2,1,0:T(1,128)} %get-tuple-element.10.pos, ...), custom_call_target="tpu_custom_call" | custom-call | tf_op jit(solution)/shard_map/rotate/pallas_call | solution.py:449
where the time goes:
time: 40.1 us; the launch traced here: 39.9 us
  Pallas kernels  38.6 us (96%)
  between operations  1.29 us (3%)
    pallas_call x1, Pallas kernels, per_device(): pl.pallas_call(functools.partial(exchange_kernel, shape, steps), grid=(st...  34.1 us
    pallas_call x1, Pallas kernels, per_device(): pl.pallas_call(functools.partial(rotate_kernel, shape, turns), out_shape=...  4.55 us

commit v1 on v0

v1 whole, which is shorter than its diff:
```python
import functools
import math

import jax
import jax.numpy as jnp
from jax import lax
from jax.experimental import pallas as pl
from jax.experimental.pallas import tpu as pltpu
from jax.sharding import PartitionSpec as P

SUB = 4
SUBSTEPS = 4
DIRECTIONS = 64

turn_angle = 130.0 * math.pi / 180.0
cos_angle = math.cos(turn_angle)
sin_angle = math.sin(turn_angle)
golden = math.pi * (3.0 - math.sqrt(5.0))
cutoff = 1.5
stiffness = 20.0
timestep = 0.05
fill_mass = 16.0
far_away = 1.0e9
MESH = pl.DeviceIdType.MESH
f32 = jnp.float32
bf16 = jnp.bfloat16
AROUND = [(a, b) for a in (-1, 0, 1) for b in (-1, 0, 1) if (a, b) != (0, 0)]
OWN = 4


def iota(shape, dim):
    return lax.broadcasted_iota(jnp.int32, shape, dim)


def slot_of(a, b):
    return (a + 1) * 3 + b + 1


def terms(value, number):
    out = []
    for _ in range(number - 1):
        part = value.astype(bf16)
        out.append(part)
        value = value - part.astype(f32)
    return out + [value.astype(bf16)]


def dot(left, right, contract=((1,), (0,))):
    return lax.dot_general(left, right, (contract, ((), ())), preferred_element_type=f32)


def wrapped(value, size):
    return jnp.where(value >= size, value - size, value)


def layer_of(row, scale, width):
    return jnp.clip(jnp.floor(row * scale).astype(jnp.int32), 0, width - 1)


def fold(values):
    row = iota(values[0].shape, 0)
    low = row < 4
    values = [
        jnp.where(low, a, b) + pltpu.roll(jnp.where(low, b, a), 4, 0)
        for a, b in zip(values[:4], values[4:])
    ]
    for dist in (2, 1):
        low = (row & dist) == 0
        values = [
            jnp.where(low, a, b) + jnp.where(low, pltpu.roll(a, 8 - dist, 0), pltpu.roll(b, dist, 0))
            for a, b in zip(values[:dist], values[dist:])
        ]
    return values[0]


def stacked(rows):
    comp = iota((8, rows[0].shape[1]), 0)
    out = jnp.zeros((8, rows[0].shape[1]), f32)
    for c, row in enumerate(rows):
        out = jnp.where(comp == c, row, out)
    return out


def axes_of(number):
    height = 1.0 - (2.0 * number + 1.0) / DIRECTIONS
    radius = jnp.sqrt(1.0 - height * height)
    phase = number * golden
    return [radius * jnp.cos(phase), radius * jnp.sin(phase), height]


def pair_sums(own_rows, source):
    dx, dy, dz = [o - s for o, s in zip(own_rows, source[:3])]
    period = source[3]
    half = 0.5 * period
    dz = dz + jnp.where(dz > half, -period, jnp.where(dz < -half, period, 0.0))
    reach = jnp.maximum(1.0 - (dx * dx + dy * dy + dz * dz), 0.0)
    weight = reach * reach
    return [weight * dx, weight * dy, weight * dz]


def force_pass(own, force, sources, first):
    slots = own.shape[1]
    wide = 32 if slots % 32 == 0 else 8

    def block(r, carry):
        at = pl.ds(pl.multiple_of(r * wide, wide), wide)
        rows = [own[c, at, :] for c in range(3)]
        total = None if first else [force[c, at, :] for c in range(3)]
        for source in sources:
            parts = pair_sums(rows, source())
            total = parts if total is None else [t + p for t, p in zip(total, parts)]
        for c in range(3):
            force[c, at, :] = total[c]
        return carry

    lax.fori_loop(0, slots // wide, block, 0)


def force_rows(force):
    slots = force.shape[1]
    comp = iota((8, slots), 0)
    out = None
    for c in range(3):
        pick = (comp == c).astype(f32).astype(bf16)
        for term in terms(force[c], 2)[::-1]:
            part = dot(pick, term, ((1,), (1,)))
            out = part if out is None else out + part
    return out


def own_columns(own, tile):
    slots = tile.shape[1]
    block = jnp.concatenate([tile, jnp.zeros((slots - 8, slots), f32)], axis=0).T
    for c in range(3):
        own[c] = jnp.broadcast_to(block[:, c : c + 1], (slots, slots))


def collide_kernel(
    shape, shift, count, solvent_hbm, occupancy_hbm, axis_hbm, pos_hbm, vel_hbm, mass_hbm,
    out, force, own, late, tiles,
    pos, vel, mass, axis, occupancy, held, acc, cell, sums, total, index, edge_x, edge_y, edge_c,
    normals, fields, halo_x, halo_y, halo_c, src,
    small_sem, chunk_sem, occ_sem, halo_send, halo_got, edge_send, edge_got, src_send, src_got,
):
    width_x, width_y, width_z = shape
    n_x, n_y = (width_x // SUB, width_y // SUB)
    rows = 2 * width_y
    slots = mass.shape[2]
    me_x, me_y = (lax.axis_index("gx"), lax.axis_index("yz"))
    size_x, size_y = (lax.axis_size("gx"), lax.axis_size("yz"))
    shift_x, shift_y, shift_z = (shift[0], shift[1], shift[2])
    high_rows = (n_y * SUB, n_y * SUB + 4)

    def device(a, b):
        return (lax.rem(me_x + a + size_x, size_x), lax.rem(me_y + b + size_y, size_y))

    def remote(source, target, send, receive, where):
        return pltpu.make_async_remote_copy(
            src_ref=source, dst_ref=target, send_sem=send, recv_sem=receive,
            device_id=where, device_id_type=MESH,
        )

    edge_c[...] = jnp.zeros_like(edge_c)
    barrier = pltpu.get_barrier_semaphore()
    for a, b in AROUND:
        pl.semaphore_signal(barrier, inc=1, device_id=device(a, b), device_id_type=MESH)

    small = [
        pltpu.make_async_copy(source, target, small_sem.at[k])
        for k, (source, target) in enumerate(
            [(pos_hbm, pos), (vel_hbm, vel), (mass_hbm, mass), (axis_hbm, axis)]
        )
    ]
    for copy in small:
        copy.start()

    def chunk(i):
        at = pl.ds(i * SUB, SUB)
        return (
            pltpu.make_async_copy(occupancy_hbm.at[at], occupancy.at[at], occ_sem.at[i]),
            pltpu.make_async_copy(solvent_hbm.at[:, at], out.at[:, at], chunk_sem.at[i]),
        )

    for i in range(n_x):
        for copy in chunk(i):
            copy.start()
    for copy in small:
        copy.wait()

    alive = iota((1, slots), 1) < count[0, 0]
    cell_x = (layer_of(pos[0, 0], SUB, width_x) + shift_x) >> 2
    cell_y = (layer_of(pos[1, 0], SUB, width_y) + shift_y) >> 2
    layer_z = layer_of(pos[2, 0], 2.0, width_z)
    cell_z = wrapped(layer_z + shift_z, width_z) >> 1
    place = cell_x * (n_y + 1) + cell_y
    weight = jnp.where(alive, mass[0], 0.0)
    comp = iota((8, slots), 0)
    four = comp & 3
    values = jnp.where(
        four == 0, vel[0, 0] * weight,
        jnp.where(four == 1, vel[1, 0] * weight, jnp.where(four == 2, vel[2, 0] * weight, weight)),
    )
    place_half = place - (comp >> 2)
    place_last = jnp.where(comp < 4, place, -1)
    tiles_y = (n_y + 2) // 2

    def in_tile(i, t):
        return (place_half if 2 * t < n_y else place_last) == i * (n_y + 1) + 2 * t

    spread = [
        jnp.where(in_tile(i, t), values, 0.0) for i in range(n_x + 1) for t in range(tiles_y)
    ]
    near = (wrapped(iota((width_z, slots), 0) + shift_z, width_z) >> 1) == cell_z
    near = near.astype(f32).astype(bf16)
    deposit = sum(
        dot(term, near, ((1,), (1,))) for term in terms(jnp.concatenate(spread, axis=0), 3)[::-1]
    )
    sums[...] = deposit.reshape(n_x + 1, tiles_y * 8, width_z)

    cell_row = wrapped(iota((width_z // 2, width_z), 1) + shift_z, width_z) >> 1
    expand = (cell_row == iota((width_z // 2, width_z), 0)).astype(f32).astype(bf16)
    number = axis[...].reshape(n_x * n_y, width_z // 2).astype(f32).astype(bf16)
    index[...] = dot(number, expand).reshape(n_x, n_y, width_z)

    start = stacked([jnp.where(alive, pos[0, 0], far_away), pos[1, 0], pos[2, 0]])
    src[0, OWN] = start * (1.0 / cutoff)

    double = (iota((rows, width_y), 0) >> 1 == iota((rows, width_y), 1)).astype(bf16)
    row = iota((8, width_z), 0)
    second = (row & 1).astype(f32)
    stays_1 = jnp.broadcast_to(shift_x, (8, width_z)) <= 2
    stays_2 = jnp.broadcast_to(shift_x, (8, width_z)) <= 1
    later = ((row >> 1) + shift_y) >= SUB
    even = ((iota((8, width_z), 1) + shift_z) & 1) == 0
    halves = jnp.where((row & 3) == 3, 0.5, 1.0)
    blank = jnp.zeros((8, width_z), f32)
    acc[...] = jnp.zeros_like(acc)

    def finish(i, ref):
        def straddling(c, j):
            now = ref[c, pl.ds(8 * j, 8), :] if j < n_y else blank
            before = ref[c, pl.ds(8 * (j - 1), 8), :] if j > 0 else blank
            return jnp.where(later, before, now)

        for t in range(tiles_y):
            blocks = [
                straddling(q & 3, 2 * t + (q >> 2)) if 2 * t + (q >> 2) <= n_y else blank
                for q in range(8)
            ]
            tile = fold(blocks) * halves
            partner = jnp.where(even, pltpu.roll(tile, width_z - 1, 1), pltpu.roll(tile, 1, 1))
            sums[i, pl.ds(8 * t, 8), :] += tile + partner

    def gather(i, carry):
        for copy in chunk(i):
            copy.wait()
        for r in range(SUB):
            held[i * SUB + r] = dot(double, occupancy[i * SUB + r].astype(f32).astype(bf16))
        for b in range(n_y):
            at = pl.ds(8 * b, 8)
            filled = [held[i * SUB + r, at, :] for r in range(SUB)]
            live = [f > second for f in filled]
            for c in range(4):
                v = filled
                if c < 3:
                    v = [jnp.where(live[r], out[c, i * SUB + r, at, :], 0.0) for r in range(SUB)]
                front = v[0] + v[1]
                back = v[3] + v[2]
                stay = jnp.where(stays_1, jnp.where(stays_2, front + v[2], front), v[0])
                move = jnp.where(stays_1, jnp.where(stays_2, v[3], back), back + v[1])
                cell[c, at, :] = acc[c, at, :] + stay
                acc[c, at, :] = move
        finish(i, cell)
        return carry

    lax.fori_loop(0, n_x, gather, 0)
    finish(n_x, acc)

    pl.semaphore_wait(barrier, len(AROUND))

    def exchange(step):
        mine = src.at[step, OWN, pl.ds(0, 4)]
        copies = {}
        for a, b in AROUND:
            k = slot_of(a, b)
            copies[k] = remote(
                mine, src.at[step, 8 - k, pl.ds(0, 4)],
                src_send.at[step, k], src_got.at[step, 8 - k], device(a, b),
            )
            copies[k].start()
        return list(copies.values())

    sends = exchange(0)

    at_low, at_high = (pl.ds(0, 4), pl.ds(n_y * SUB, 4))
    every = pl.ds(0, n_x + 1)
    halo = [
        (sums.at[n_x], halo_x.at[0], (1, 0)),
        (sums.at[0], halo_x.at[1], (-1, 0)),
        (sums.at[every, at_high], halo_y.at[0, every, at_low], (0, 1)),
        (sums.at[every, at_low], halo_y.at[1, every, at_low], (0, -1)),
        (sums.at[n_x, at_high], halo_c.at[0, at_low], (1, 1)),
        (sums.at[n_x, at_low], halo_c.at[1, at_low], (1, -1)),
        (sums.at[0, at_high], halo_c.at[2, at_low], (-1, 1)),
        (sums.at[0, at_low], halo_c.at[3, at_low], (-1, -1)),
    ]
    halo = [
        remote(source, target, halo_send.at[k], halo_got.at[k], device(*where))
        for k, (source, target, where) in enumerate(halo)
    ]
    for copy in halo:
        copy.start()
    edges = [
        (index.at[0], edge_x, (-1, 0)),
        (index.at[pl.ds(0, n_x), 0], edge_y, (0, -1)),
        (index.at[0, pl.ds(0, 1)], edge_c.at[pl.ds(0, 1)], (-1, -1)),
    ]
    edges = [
        remote(source, target, edge_send.at[k], edge_got.at[k], device(*where))
        for k, (source, target, where) in enumerate(edges)
    ]
    for copy in edges:
        copy.start()

    period = (width_z // 2) / cutoff
    step_x, step_y = (n_x / cutoff, n_y / cutoff)
    side = 1 - 2 * (me_x & 1)
    quick, slow = (side, -side)

    def source(step, a, b):
        slot = slot_of(a, b)
        offset = None if isinstance(a, int) else a.astype(f32) * step_x

        def read():
            x, y, z = [src[step, slot, pl.ds(c, 1), :] for c in range(3)]
            x = x if offset is None else x + offset
            return (x, y if b == 0 else y + b * step_y, z, period)

        return read

    def arrived(step, a, b):
        slot = slot_of(a, b)
        remote(
            src.at[step, OWN, pl.ds(0, 4)], src.at[step, slot, pl.ds(0, 4)],
            src_send.at[step, slot], src_got.at[step, slot], device(0, 1),
        ).wait_recv()

    def early_forces(step):
        for b in (-1, 1):
            arrived(step, 0, b)
        force_pass(own, force, [source(step, 0, b) for b in (0, -1, 1)], True)
        for b in (-1, 0, 1):
            arrived(step, quick, b)
        force_pass(own, force, [source(step, quick, b) for b in (-1, 0, 1)], False)

    def late_arrivals(step):
        for b in (-1, 0, 1):
            arrived(step, slow, b)

    def late_forces(step):
        late_arrivals(step)
        force_pass(own, force, [source(step, slow, b) for b in (-1, 0, 1)], False)
        return force_rows(force)

    own_columns(own, src[0, OWN])
    early_forces(0)
    push = late_forces(0)

    for copy in halo:
        copy.wait_recv()
    total[...] = sums[...]
    total[0] += halo_x[0]
    total[n_x] += halo_x[1]
    for i in range(n_x + 1):
        total[i, at_low, :] += halo_y[0, i, at_low, :]
        total[i, at_high, :] += halo_y[1, i, at_low, :]
    total[0, at_low, :] += halo_c[0, at_low, :]
    total[0, at_high, :] += halo_c[1, at_low, :]
    total[n_x, at_low, :] += halo_c[2, at_low, :]
    total[n_x, at_high, :] += halo_c[3, at_low, :]
    for copy in edges:
        copy.wait_recv()

    chosen = (iota((width_z, slots), 0) == layer_z).astype(f32).astype(bf16)
    block = total[...].reshape((n_x + 1) * tiles_y * 8, width_z)
    at_z = sum(dot(term, chosen) for term in terms(block, 2)[::-1])
    picked = jnp.zeros((8, slots), f32)
    for i in range(n_x + 1):
        for t in range(tiles_y):
            n = 8 * (i * tiles_y + t)
            picked = picked + jnp.where(in_tile(i, t), at_z[n : n + 8], 0.0)
    picked = picked + pltpu.roll(picked, 4, 0)
    numbers = jnp.concatenate(
        [index[...].reshape(n_x * n_y, width_z), edge_x[...], edge_y[...], edge_c[...]], axis=0
    )
    at_z = dot(numbers.astype(bf16), chosen)
    wanted = [place - comp == i * (n_y + 1) for i in range(n_x + 1)]
    wanted.append(place - comp * (n_y + 1) == n_y)
    wanted.append(jnp.logical_and(comp == 0, place == n_x * (n_y + 1) + n_y))
    found = jnp.zeros((8, slots), f32)
    for n, mask in enumerate(wanted):
        found = found + jnp.where(mask, at_z[8 * n : 8 * n + 8], 0.0)
    found = jnp.sum(found, axis=0, keepdims=True)
    heavy = jnp.maximum(picked[3:4], fill_mass)
    mean = [picked[c : c + 1] / heavy for c in range(3)]
    n = axes_of(found)
    rel = [vel[c, 0] - mean[c] for c in range(3)]
    cross = [n[1] * rel[2] - n[2] * rel[1], n[2] * rel[0] - n[0] * rel[2], n[0] * rel[1] - n[1] * rel[0]]
    along = n[0] * rel[0] + n[1] * rel[1] + n[2] * rel[2]
    speed = stacked([
        mean[c] + cos_angle * rel[c] + sin_angle * cross[c] + (1.0 - cos_angle) * along * n[c]
        for c in range(3)
    ])
    kick = jnp.broadcast_to((timestep * stiffness * cutoff) / mass[0], (8, slots))
    place_now = start

    def cell_fields(i, rows_of):
        for b in range(n_y):
            pair = [
                [jnp.where(later, total[i, pl.ds(4 * (b + 1) + c, 1), :], total[i, pl.ds(4 * b + c, 1), :])
                 for c in range(4)],
                [jnp.where(later, normals[c, pl.ds(rows_of(b + 1), 1), :], normals[c, pl.ds(rows_of(b), 1), :])
                 for c in range(3)],
            ]
            scale = 1.0 / jnp.maximum(pair[0][3], fill_mass)
            for c in range(3):
                fields[i, b, c] = pair[0][c] * scale
                fields[i, b, 3 + c] = pair[1][c]

    def turn(x, carry):
        at_cell = (x + shift_x) >> 2
        for b in range(n_y):
            at = pl.ds(8 * b, 8)
            mean = [fields[at_cell, b, c] for c in range(3)]
            n = [fields[at_cell, b, 3 + c] for c in range(3)]
            old = [out[c, x, at, :] for c in range(3)]
            rel = [old[c] - mean[c] for c in range(3)]
            along = (1.0 - cos_angle) * (n[0] * rel[0] + n[1] * rel[1] + n[2] * rel[2])
            cross = [
                n[1] * rel[2] - n[2] * rel[1],
                n[2] * rel[0] - n[0] * rel[2],
                n[0] * rel[1] - n[1] * rel[0],
            ]
            live = held[x, at, :] > second
            for c in range(3):
                new = mean[c] + cos_angle * rel[c] + sin_angle * cross[c] + along * n[c]
                out[c, x, at, :] = jnp.where(live, new, old[c])
        return carry

    def idle_work(step):
        if step == 1:
            for c, part in enumerate(axes_of(numbers)):
                normals[c] = part

            def inner(i, carry):
                cell_fields(i, lambda b: i * n_y + b if b < n_y else n_x * n_y + 8 + i)
                return carry

            lax.fori_loop(0, n_x, inner, 0)
            cell_fields(n_x, lambda b: n_x * n_y + b if b < n_y else n_x * n_y + 16)
            lax.fori_loop(0, width_x // 2, turn, 0)
        if step == 2:
            lax.fori_loop(width_x // 2, width_x, turn, 0)

    for step in range(1, SUBSTEPS):
        speed = speed + push * kick
        place_now = place_now + timestep * speed
        src[step, OWN] = place_now * (1.0 / cutoff)
        sends = sends + exchange(step)
        own_columns(own, src[step, OWN])
        idle_work(step)
        early_forces(step)
        if step < SUBSTEPS - 1:
            push = late_forces(step)

    tiles[0] = place_now
    tiles[1] = speed
    tiles[2] = kick
    tiles[3] = stacked([pos[c, 0] for c in range(3)])
    tiles[4] = stacked([vel[c, 0] for c in range(3)])
    tiles[5] = jnp.broadcast_to(jnp.where(alive, 1.0, 0.0), (8, slots))
    late_arrivals(SUBSTEPS - 1)
    for b in (-1, 0, 1):
        x, y, z, _ = source(SUBSTEPS - 1, slow, b)()
        late[b + 1] = stacked([x, y, z])
    for copy in sends + halo + edges:
        copy.wait_send()


def finish_kernel(shape, turned, force, own, late, tiles, out, pos_out, vel_out, sem):
    width_x, width_y, width_z = shape
    parts = 2
    thin = width_x // parts
    copies = []
    for c in range(3):
        for h in range(parts):
            at = pl.ds(h * thin, thin)
            copies.append(
                pltpu.make_async_copy(turned.at[c, at], out.at[c, at], sem.at[c * parts + h])
            )
            copies[-1].start()

    period = (width_z // 2) / cutoff

    def source(k):
        return lambda: tuple(late[k, pl.ds(c, 1), :] for c in range(3)) + (period,)

    force_pass(own, force, [source(k) for k in range(3)], False)
    push = force_rows(force)
    speed = tiles[1] + push * tiles[2]
    place = tiles[0] + timestep * speed
    alive = tiles[5] > 0
    place = jnp.where(alive, place, tiles[3])
    speed = jnp.where(alive, speed, tiles[4])
    for c in range(3):
        pos_out[c, 0] = place[c : c + 1]
        vel_out[c, 0] = speed[c : c + 1]
    for copy in copies:
        copy.wait()


def per_device(
    solvent_vel, occupancy, grid_shift, axis_index, colloid_pos, colloid_vel, colloid_mass, colloid_count
):
    shape = occupancy.shape
    width_x, width_y, width_z = shape
    rows = 2 * width_y
    n_x, n_y = (width_x // SUB, width_y // SUB)
    slots = colloid_mass.shape[2]
    solvent = solvent_vel.reshape(3, width_x, rows, width_z)
    smem = pl.BlockSpec(memory_space=pltpu.SMEM)
    vmem = pl.BlockSpec(memory_space=pltpu.VMEM)
    hbm = pl.BlockSpec(memory_space=pltpu.HBM)
    tall = (n_y + 2) // 2 * 8
    dma = pltpu.SemaphoreType.DMA

    def in_hbm(x):
        return pltpu.with_memory_space_constraint(x, pltpu.HBM)

    turned, force, own, late, tiles = pl.pallas_call(
        functools.partial(collide_kernel, shape),
        out_shape=[
            pltpu.VMEM(solvent.shape, f32),
            pltpu.VMEM((3, slots, slots), f32),
            pltpu.VMEM((3, slots, slots), f32),
            pltpu.VMEM((3, 8, slots), f32),
            pltpu.VMEM((6, 8, slots), f32),
        ],
        in_specs=[smem, smem] + [hbm] * 6,
        out_specs=[vmem] * 5,
        scratch_shapes=[
            pltpu.VMEM(colloid_pos.shape, f32),
            pltpu.VMEM(colloid_vel.shape, f32),
            pltpu.VMEM(colloid_mass.shape, f32),
            pltpu.VMEM(axis_index.shape, jnp.int32),
            pltpu.VMEM(shape, jnp.int32),
            pltpu.VMEM((width_x, rows, width_z), f32),
            pltpu.VMEM((4, rows, width_z), f32),
            pltpu.VMEM((4, rows, width_z), f32),
            pltpu.VMEM((n_x + 1, tall, width_z), f32),
            pltpu.VMEM((n_x + 1, tall, width_z), f32),
            pltpu.VMEM((n_x, n_y, width_z), f32),
            pltpu.VMEM((8, width_z), f32),
            pltpu.VMEM((8, width_z), f32),
            pltpu.VMEM((8, width_z), f32),
            pltpu.VMEM((3, n_x * n_y + 24, width_z), f32),
            pltpu.VMEM((n_x + 1, n_y, 6, 8, width_z), f32),
            pltpu.VMEM((2, tall, width_z), f32),
            pltpu.VMEM((2, n_x + 1, 8, width_z), f32),
            pltpu.VMEM((4, 8, width_z), f32),
            pltpu.VMEM((SUBSTEPS, 9, 8, slots), f32),
            dma((4,)),
            dma((n_x,)),
            dma((n_x,)),
            dma((8,)),
            dma((8,)),
            dma((3,)),
            dma((3,)),
            dma((SUBSTEPS, 9)),
            dma((SUBSTEPS, 9)),
        ],
        compiler_params=pltpu.CompilerParams(
            collective_id=0, has_side_effects=True, vmem_limit_bytes=32 * 2**20
        ),
        name="collide",
    )(
        grid_shift, colloid_count, in_hbm(solvent), in_hbm(occupancy), in_hbm(axis_index),
        in_hbm(colloid_pos), in_hbm(colloid_vel), in_hbm(colloid_mass),
    )

    parts = 2
    solvent_out, pos_out, vel_out = pl.pallas_call(
        functools.partial(finish_kernel, shape),
        out_shape=[
            jax.ShapeDtypeStruct(solvent.shape, f32),
            jax.ShapeDtypeStruct(colloid_pos.shape, f32),
            jax.ShapeDtypeStruct(colloid_vel.shape, f32),
        ],
        in_specs=[vmem] * 5,
        out_specs=[hbm, vmem, vmem],
        scratch_shapes=[dma((3 * parts,))],
        input_output_aliases={},
        compiler_params=pltpu.CompilerParams(vmem_limit_bytes=8 * 2**20),
        name="finish",
    )(turned, force, own, late, tiles)
    return (solvent_out.reshape(solvent_vel.shape), pos_out, vel_out)


def solution(mesh):
    return jax.shard_map(
        per_device,
        mesh=mesh,
        in_specs=(
            P(None, "gx", "yz", None, None),
            P("gx", "yz", None),
            P(),
            P("gx", "yz", None),
            P(None, "gx", "yz", None),
            P(None, "gx", "yz", None),
            P("gx", "yz", None),
            P("gx", "yz"),
        ),
        out_specs=(
            P(None, "gx", "yz", None, None),
            P(None, "gx", "yz", None),
            P(None, "gx", "yz", None),
        ),
        check_vma=False,
    )
```

time: 40.1 us -> 31.5 us (0.79)
  Pallas kernels: 38.6 us -> 29.4 us
  local copies, waits for them, and re-layouts: 0 us -> 0.65 us
    pallas_call x2, Pallas kernels: 38.6 us -> 29.4 us  [the longest x1 27.2 us: per_device(): pl.pallas_call(functools.partial(collide_kernel, shape), out_shape=[pltpu...]
    unnamed x0 -> x2, local copies, waits for them, and re-layouts: none -> 0.65 us
where the time goes in v1:
time: 31.5 us; the launch traced here: 31.4 us
  Pallas kernels  29.4 us (93%)
  between operations  1.3 us (4%)
  local copies, waits for them, and re-layouts  0.65 us (2%)
    pallas_call x1, Pallas kernels, per_device(): pl.pallas_call(functools.partial(collide_kernel, shape), out_shape=[pltpu...  27.2 us
    pallas_call x1, Pallas kernels, per_device(): pl.pallas_call(functools.partial(finish_kernel, shape), out_shape=[jax.Sh...  2.28 us
    unnamed x2, local copies, waits for them, and re-layouts  0.65 us

profile of v1, /device:TPU:0, one launch (start us, length us, event | category | flops | bytes accessed | tf_op | source)
XLA Modules:
  0.0 31.4 jit_solution(188948165872963628)
XLA Ops:
  1.3 0.0 copy-start
  1.3 0.6 %copy-done = s32[3]{0:T(128)S(1)} copy-done((s32[3]{0:T(128)S(1)}, s32[3]{0:T(128)}, u32[]{:S(2)}) %copy-start) | copy-done | bytes 36
  1.9 27.2 %collide.1 = (f32[3,32,64,128]{3,2,1,0:T(8,128)S(1)}, f32[3,128,128]{2,1,0:T(8,128)S(1)}, f32[3,128,128]{2,1,0:T(8,128)S(1)}, f32[3,8,128]{2,1,0:T(8,128)S(1)}, f32[6,8,128]{2,1,0:T(8,128)S(1)}) custom-call(s32[3]{0:T(128)S(1)} %copy-done, s32[1,1]{1,0:T(1,128)S(6)} %copy.11.count, f32[3,32,64,128]{3,2,1,0:T(8,128)} %bitcast.2, ...), custom_call_target="tpu_custom_call" | custom-call | tf_op jit(solution)/shard_map/collide/pallas_call | solution.py:540
  29.1 2.3 %finish.1 = (f32[3,32,64,128]{3,2,1,0:T(8,128)}, f32[3,1,1,128]{3,2,1,0:T(1,128)}, f32[3,1,1,128]{3,2,1,0:T(1,128)}) custom-call(f32[3,32,64,128]{3,2,1,0:T(8,128)S(1)} %get-tuple-element.11.turned, f32[3,128,128]{2,1,0:T(8,128)S(1)} %get-tuple-element.12.force, f32[3,128,128]{2,1,0:T(8,128)S(1)} %get-tuple-element.13.own, ...), custom_call_target="tpu_custom_call" | custom-call | tf_op jit(solution)/shard_map/finish/pallas_call | solution.py:592
Async XLA Ops:
  1.3 0.7 %copy-start = (s32[3]{0:T(128)S(1)}, s32[3]{0:T(128)}, u32[]{:S(2)}) copy-start(s32[3]{0:T(128)} %shift.1) | copy-start | bytes 40

commit v2 on v1

--- a/solution.py
+++ b/solution.py
@@ -136,11 +136,11 @@
 
 
 def collide_kernel(
-    shape, shift, count, solvent_hbm, occupancy_hbm, axis_hbm, pos_hbm, vel_hbm, mass_hbm,
+    shape, shift_hbm, count, solvent_hbm, occupancy_hbm, axis_hbm, pos_hbm, vel_hbm, mass_hbm,
     out, force, own, late, tiles,
-    pos, vel, mass, axis, occupancy, held, acc, cell, sums, total, index, edge_x, edge_y, edge_c,
+    shift, pos, vel, mass, axis, occupancy, held, cell, sums, total, index, edge_x, edge_y, edge_c,
     normals, fields, halo_x, halo_y, halo_c, src,
-    small_sem, chunk_sem, occ_sem, halo_send, halo_got, edge_send, edge_got, src_send, src_got,
+    small_sem, chunk_sem, halo_send, halo_got, edge_send, edge_got, src_send, src_got,
 ):
     width_x, width_y, width_z = shape
     n_x, n_y = (width_x // SUB, width_y // SUB)
@@ -148,8 +148,6 @@
     slots = mass.shape[2]
     me_x, me_y = (lax.axis_index("gx"), lax.axis_index("yz"))
     size_x, size_y = (lax.axis_size("gx"), lax.axis_size("yz"))
-    shift_x, shift_y, shift_z = (shift[0], shift[1], shift[2])
-    high_rows = (n_y * SUB, n_y * SUB + 4)
 
     def device(a, b):
         return (lax.rem(me_x + a + size_x, size_x), lax.rem(me_y + b + size_y, size_y))
@@ -168,24 +166,23 @@
     small = [
         pltpu.make_async_copy(source, target, small_sem.at[k])
         for k, (source, target) in enumerate(
-            [(pos_hbm, pos), (vel_hbm, vel), (mass_hbm, mass), (axis_hbm, axis)]
+            [
+                (shift_hbm, shift), (pos_hbm, pos), (vel_hbm, vel),
+                (mass_hbm, mass), (axis_hbm, axis), (occupancy_hbm, occupancy),
+            ]
         )
     ]
-    for copy in small:
+    chunks = [
+        pltpu.make_async_copy(
+            solvent_hbm.at[:, pl.ds(i * SUB, SUB)], out.at[:, pl.ds(i * SUB, SUB)], chunk_sem.at[i]
+        )
+        for i in range(n_x)
+    ]
+    for copy in small + chunks:
         copy.start()
-
-    def chunk(i):
-        at = pl.ds(i * SUB, SUB)
-        return (
-            pltpu.make_async_copy(occupancy_hbm.at[at], occupancy.at[at], occ_sem.at[i]),
-            pltpu.make_async_copy(solvent_hbm.at[:, at], out.at[:, at], chunk_sem.at[i]),
-        )
-
-    for i in range(n_x):
-        for copy in chunk(i):
-            copy.start()
-    for copy in small:
+    for copy in small[:-1]:
         copy.wait()
+    shift_x, shift_y, shift_z = (shift[0], shift[1], shift[2])
 
     alive = iota((1, slots), 1) < count[0, 0]
     cell_x = (layer_of(pos[0, 0], SUB, width_x) + shift_x) >> 2
@@ -225,7 +222,12 @@
     start = stacked([jnp.where(alive, pos[0, 0], far_away), pos[1, 0], pos[2, 0]])
     src[0, OWN] = start * (1.0 / cutoff)
 
-    double = (iota((rows, width_y), 0) >> 1 == iota((rows, width_y), 1)).astype(bf16)
+    double = (iota((SUB * rows, SUB * width_y), 0) >> 1 == iota((SUB * rows, SUB * width_y), 1)).astype(bf16)
+    small[-1].wait()
+    for i in range(n_x):
+        at = pl.ds(i * SUB, SUB)
+        filled = occupancy[at].reshape(SUB * width_y, width_z).astype(f32).astype(bf16)
+        held[at] = dot(double, filled).reshape(SUB, rows, width_z)
     row = iota((8, width_z), 0)
     second = (row & 1).astype(f32)
     stays_1 = jnp.broadcast_to(shift_x, (8, width_z)) <= 2
@@ -234,12 +236,11 @@
     even = ((iota((8, width_z), 1) + shift_z) & 1) == 0
     halves = jnp.where((row & 3) == 3, 0.5, 1.0)
     blank = jnp.zeros((8, width_z), f32)
-    acc[...] = jnp.zeros_like(acc)
-
-    def finish(i, ref):
+
+    def finish(i):
         def straddling(c, j):
-            now = ref[c, pl.ds(8 * j, 8), :] if j < n_y else blank
-            before = ref[c, pl.ds(8 * (j - 1), 8), :] if j > 0 else blank
+            now = cell[i, c, pl.ds(8 * j, 8), :] if j < n_y else blank
+            before = cell[i, c, pl.ds(8 * (j - 1), 8), :] if j > 0 else blank
             return jnp.where(later, before, now)
 
         for t in range(tiles_y):
@@ -251,11 +252,7 @@
             partner = jnp.where(even, pltpu.roll(tile, width_z - 1, 1), pltpu.roll(tile, 1, 1))
             sums[i, pl.ds(8 * t, 8), :] += tile + partner
 
-    def gather(i, carry):
-        for copy in chunk(i):
-            copy.wait()
-        for r in range(SUB):
-            held[i * SUB + r] = dot(double, occupancy[i * SUB + r].astype(f32).astype(bf16))
+    def gather(i):
         for b in range(n_y):
             at = pl.ds(8 * b, 8)
             filled = [held[i * SUB + r, at, :] for r in range(SUB)]
@@ -268,13 +265,16 @@
                 back = v[3] + v[2]
                 stay = jnp.where(stays_1, jnp.where(stays_2, front + v[2], front), v[0])
                 move = jnp.where(stays_1, jnp.where(stays_2, v[3], back), back + v[1])
-                cell[c, at, :] = acc[c, at, :] + stay
-                acc[c, at, :] = move
-        finish(i, cell)
-        return carry
-
-    lax.fori_loop(0, n_x, gather, 0)
-    finish(n_x, acc)
+                cell[i, c, at, :] = stay if i == 0 else cell[i, c, at, :] + stay
+                cell[i + 1, c, at, :] = move
+
+    for i in range(n_x):
+        chunks[i].wait()
+        gather(i)
+        if i > 0:
+            finish(i - 1)
+    finish(n_x - 1)
+    finish(n_x)
 
     pl.semaphore_wait(barrier, len(AROUND))
 
@@ -546,17 +546,17 @@
             pltpu.VMEM((3, 8, slots), f32),
             pltpu.VMEM((6, 8, slots), f32),
         ],
-        in_specs=[smem, smem] + [hbm] * 6,
+        in_specs=[hbm, smem] + [hbm] * 6,
         out_specs=[vmem] * 5,
         scratch_shapes=[
+            pltpu.SMEM(grid_shift.shape, jnp.int32),
             pltpu.VMEM(colloid_pos.shape, f32),
             pltpu.VMEM(colloid_vel.shape, f32),
             pltpu.VMEM(colloid_mass.shape, f32),
             pltpu.VMEM(axis_index.shape, jnp.int32),
             pltpu.VMEM(shape, jnp.int32),
             pltpu.VMEM((width_x, rows, width_z), f32),
-            pltpu.VMEM((4, rows, width_z), f32),
-            pltpu.VMEM((4, rows, width_z), f32),
+            pltpu.VMEM((n_x + 1, 4, rows, width_z), f32),
             pltpu.VMEM((n_x + 1, tall, width_z), f32),
             pltpu.VMEM((n_x + 1, tall, width_z), f32),
             pltpu.VMEM((n_x, n_y, width_z), f32),
@@ -569,8 +569,7 @@
             pltpu.VMEM((2, n_x + 1, 8, width_z), f32),
             pltpu.VMEM((4, 8, width_z), f32),
             pltpu.VMEM((SUBSTEPS, 9, 8, slots), f32),
-            dma((4,)),
-            dma((n_x,)),
+            dma((6,)),
             dma((n_x,)),
             dma((8,)),
             dma((8,)),
@@ -584,7 +583,7 @@
         ),
         name="collide",
     )(
-        grid_shift, colloid_count, in_hbm(solvent), in_hbm(occupancy), in_hbm(axis_index),
+        in_hbm(grid_shift), colloid_count, in_hbm(solvent), in_hbm(occupancy), in_hbm(axis_index),
         in_hbm(colloid_pos), in_hbm(colloid_vel), in_hbm(colloid_mass),
     )
 

time: 31.5 us -> 29.4 us (0.933)
  Pallas kernels: 29.4 us -> 28 us
  local copies, waits for them, and re-layouts: 0.65 us -> 0 us
    pallas_call x1, Pallas kernels: 27.2 us -> 25.7 us  [per_device(): pl.pallas_call(functools.partial(collide_kernel, shape), out_shape=[pltpu...]
    unnamed x2 -> x0, local copies, waits for them, and re-layouts: 0.65 us -> none
where the time goes in v2:
time: 29.4 us; the launch traced here: 29.3 us
  Pallas kernels  28 us (95%)
  between operations  1.29 us (4%)
    pallas_call x1, Pallas kernels, per_device(): pl.pallas_call(functools.partial(collide_kernel, shape), out_shape=[pltpu...  25.7 us
    pallas_call x1, Pallas kernels, per_device(): pl.pallas_call(functools.partial(finish_kernel, shape), out_shape=[jax.Sh...  2.28 us

profile of v2, /device:TPU:0, one launch (start us, length us, event | category | flops | bytes accessed | tf_op | source)
XLA Modules:
  0.0 29.3 jit_solution(3432305483557176033)
XLA Ops:
  1.3 25.7 %collide.1 = (f32[3,32,64,128]{3,2,1,0:T(8,128)S(1)}, f32[3,128,128]{2,1,0:T(8,128)S(1)}, f32[3,128,128]{2,1,0:T(8,128)S(1)}, f32[3,8,128]{2,1,0:T(8,128)S(1)}, f32[6,8,128]{2,1,0:T(8,128)S(1)}) custom-call(s32[3]{0:T(128)} %shift_hbm.1, s32[1,1]{1,0:T(1,128)S(6)} %copy.11.count, f32[3,32,64,128]{3,2,1,0:T(8,128)} %bitcast.2, s32[32,32,128]{2,1,0:T(8,128)} %occupancy_hbm.1, ...), custom_call_target="tpu_custom_call" | custom-call | tf_op jit(solution)/shard_map/collide/pallas_call | solution.py:540
  27.0 2.3 %finish.1 = (f32[3,32,64,128]{3,2,1,0:T(8,128)}, f32[3,1,1,128]{3,2,1,0:T(1,128)}, f32[3,1,1,128]{3,2,1,0:T(1,128)}) custom-call(f32[3,32,64,128]{3,2,1,0:T(8,128)S(1)} %get-tuple-element.11.turned, f32[3,128,128]{2,1,0:T(8,128)S(1)} %get-tuple-element.12.force, f32[3,128,128]{2,1,0:T(8,128)S(1)} %get-tuple-element.13.own, ...), custom_call_target="tpu_custom_call" | custom-call | tf_op jit(solution)/shard_map/finish/pallas_call | solution.py:591

commit v3 on v2

--- a/solution.py
+++ b/solution.py
@@ -24,7 +24,9 @@
 MESH = pl.DeviceIdType.MESH
 f32 = jnp.float32
 bf16 = jnp.bfloat16
-AROUND = [(a, b) for a in (-1, 0, 1) for b in (-1, 0, 1) if (a, b) != (0, 0)]
+RING = [(a, b) for a in (-1, 0, 1) for b in (-1, 0, 1)]
+AROUND = [pair for pair in RING if pair != (0, 0)]
+WIDE = [(a, b) for a in (-1, 1, -2, 2, 0) for b in (-1, 0, 1, -2, 2) if (a, b) != (0, 0)]
 OWN = 4
 
 
@@ -34,6 +36,10 @@
 
 def slot_of(a, b):
     return (a + 1) * 3 + b + 1
+
+
+def wide_slot(a, b):
+    return (a + 2) * 5 + b + 2
 
 
 def terms(value, number):
@@ -137,10 +143,11 @@
 
 def collide_kernel(
     shape, shift_hbm, count, solvent_hbm, occupancy_hbm, axis_hbm, pos_hbm, vel_hbm, mass_hbm,
-    out, force, own, late, tiles,
+    out, first, second, third, tiles,
     shift, pos, vel, mass, axis, occupancy, held, cell, sums, total, index, edge_x, edge_y, edge_c,
-    normals, fields, halo_x, halo_y, halo_c, src,
+    normals, fields, halo_x, halo_y, halo_c, src, wide, force, own,
     small_sem, chunk_sem, halo_send, halo_got, edge_send, edge_got, src_send, src_got,
+    wide_send, wide_got,
 ):
     width_x, width_y, width_z = shape
     n_x, n_y = (width_x // SUB, width_y // SUB)
@@ -160,7 +167,7 @@
 
     edge_c[...] = jnp.zeros_like(edge_c)
     barrier = pltpu.get_barrier_semaphore()
-    for a, b in AROUND:
+    for a, b in WIDE:
         pl.semaphore_signal(barrier, inc=1, device_id=device(a, b), device_id_type=MESH)
 
     small = [
@@ -220,7 +227,8 @@
     index[...] = dot(number, expand).reshape(n_x, n_y, width_z)
 
     start = stacked([jnp.where(alive, pos[0, 0], far_away), pos[1, 0], pos[2, 0]])
-    src[0, OWN] = start * (1.0 / cutoff)
+    kick = jnp.broadcast_to((timestep * stiffness * cutoff) / mass[0], (8, slots))
+    src[0, OWN] = jnp.where(comp == 3, kick, start * (1.0 / cutoff))
 
     double = (iota((SUB * rows, SUB * width_y), 0) >> 1 == iota((SUB * rows, SUB * width_y), 1)).astype(bf16)
     small[-1].wait()
@@ -229,7 +237,7 @@
         filled = occupancy[at].reshape(SUB * width_y, width_z).astype(f32).astype(bf16)
         held[at] = dot(double, filled).reshape(SUB, rows, width_z)
     row = iota((8, width_z), 0)
-    second = (row & 1).astype(f32)
+    odd = (row & 1).astype(f32)
     stays_1 = jnp.broadcast_to(shift_x, (8, width_z)) <= 2
     stays_2 = jnp.broadcast_to(shift_x, (8, width_z)) <= 1
     later = ((row >> 1) + shift_y) >= SUB
@@ -256,7 +264,7 @@
         for b in range(n_y):
             at = pl.ds(8 * b, 8)
             filled = [held[i * SUB + r, at, :] for r in range(SUB)]
-            live = [f > second for f in filled]
+            live = [f > odd for f in filled]
             for c in range(4):
                 v = filled
                 if c < 3:
@@ -276,7 +284,7 @@
     finish(n_x - 1)
     finish(n_x)
 
-    pl.semaphore_wait(barrier, len(AROUND))
+    pl.semaphore_wait(barrier, len(WIDE))
 
     def exchange(step):
         mine = src.at[step, OWN, pl.ds(0, 4)]
@@ -411,7 +419,6 @@
         mean[c] + cos_angle * rel[c] + sin_angle * cross[c] + (1.0 - cos_angle) * along * n[c]
         for c in range(3)
     ])
-    kick = jnp.broadcast_to((timestep * stiffness * cutoff) / mass[0], (8, slots))
     place_now = start
 
     def cell_fields(i, rows_of):
@@ -441,7 +448,7 @@
                 n[2] * rel[0] - n[0] * rel[2],
                 n[0] * rel[1] - n[1] * rel[0],
             ]
-            live = held[x, at, :] > second
+            live = held[x, at, :] > odd
             for c in range(3):
                 new = mean[c] + cos_angle * rel[c] + sin_angle * cross[c] + along * n[c]
                 out[c, x, at, :] = jnp.where(live, new, old[c])
@@ -462,56 +469,120 @@
         if step == 2:
             lax.fori_loop(width_x // 2, width_x, turn, 0)
 
-    for step in range(1, SUBSTEPS):
-        speed = speed + push * kick
-        place_now = place_now + timestep * speed
-        src[step, OWN] = place_now * (1.0 / cutoff)
-        sends = sends + exchange(step)
-        own_columns(own, src[step, OWN])
-        idle_work(step)
-        early_forces(step)
-        if step < SUBSTEPS - 1:
-            push = late_forces(step)
-
+    speed = speed + push * kick
+    place_now = place_now + timestep * speed
+    src[1, OWN] = place_now * (1.0 / cutoff)
+    sends = sends + exchange(1)
+    own_columns(own, src[1, OWN])
+    idle_work(1)
+    early_forces(1)
+    push = late_forces(1)
+
+    speed = speed + push * kick
+    place_now = place_now + timestep * speed
+    mine = wide_slot(0, 0)
+    wide[mine] = place_now * (1.0 / cutoff)
+    spread = []
+    for a, b in WIDE:
+        k = wide_slot(a, b)
+        spread.append(
+            remote(
+                wide.at[mine, pl.ds(0, 4)], wide.at[24 - k, pl.ds(0, 4)],
+                wide_send.at[k], wide_got.at[24 - k], device(a, b),
+            )
+        )
+    for copy in spread:
+        copy.start()
+    idle_work(2)
+    first[...] = src[0]
+    second[...] = src[1]
     tiles[0] = place_now
     tiles[1] = speed
-    tiles[2] = kick
-    tiles[3] = stacked([pos[c, 0] for c in range(3)])
-    tiles[4] = stacked([vel[c, 0] for c in range(3)])
-    tiles[5] = jnp.broadcast_to(jnp.where(alive, 1.0, 0.0), (8, slots))
-    late_arrivals(SUBSTEPS - 1)
-    for b in (-1, 0, 1):
-        x, y, z, _ = source(SUBSTEPS - 1, slow, b)()
-        late[b + 1] = stacked([x, y, z])
-    for copy in sends + halo + edges:
+    tiles[2] = stacked([pos[c, 0] for c in range(3)])
+    tiles[3] = stacked([vel[c, 0] for c in range(3)])
+    tiles[4] = jnp.broadcast_to(jnp.where(alive, 1.0, 0.0), (8, slots))
+    for copy in spread:
+        copy.wait_recv()
+    third[...] = wide[...]
+    for copy in sends + halo + edges + spread:
         copy.wait_send()
 
 
-def finish_kernel(shape, turned, force, own, late, tiles, out, pos_out, vel_out, sem):
+def finish_kernel(
+    shape, turned, first, second, third, tiles, out, pos_out, vel_out, own, force, later, sem
+):
     width_x, width_y, width_z = shape
-    parts = 2
-    thin = width_x // parts
+    n_x, n_y = (width_x // SUB, width_y // SUB)
+    slots = first.shape[2]
     copies = []
     for c in range(3):
-        for h in range(parts):
-            at = pl.ds(h * thin, thin)
-            copies.append(
-                pltpu.make_async_copy(turned.at[c, at], out.at[c, at], sem.at[c * parts + h])
-            )
-            copies[-1].start()
+        copies.append(pltpu.make_async_copy(turned.at[c], out.at[c], sem.at[c]))
+        copies[-1].start()
 
     period = (width_z // 2) / cutoff
-
-    def source(k):
-        return lambda: tuple(late[k, pl.ds(c, 1), :] for c in range(3)) + (period,)
-
-    force_pass(own, force, [source(k) for k in range(3)], False)
-    push = force_rows(force)
-    speed = tiles[1] + push * tiles[2]
-    place = tiles[0] + timestep * speed
-    alive = tiles[5] > 0
-    place = jnp.where(alive, place, tiles[3])
-    speed = jnp.where(alive, speed, tiles[4])
+    step_x, step_y = (n_x / cutoff, n_y / cutoff)
+    lane = iota((slots, slots), 1)
+    block = 16 if slots % 16 == 0 else 8
+
+    def columns(group):
+        pad = jnp.zeros((slots - 8 * len(group), slots), f32)
+        flipped = jnp.concatenate(group + [pad], axis=0).T
+        for n in range(len(group)):
+            for c in range(3):
+                own[n, c] = jnp.broadcast_to(flipped[:, 8 * n + c : 8 * n + c + 1], (slots, slots))
+
+    def pushes(n, trips, sources):
+        def body(r, carry):
+            at = pl.ds(pl.multiple_of(r * block, block), block)
+            rows = [own[n, c, at, :] for c in range(3)]
+            total = None
+            for ref, k, a, b in sources:
+                x, y, z = [ref[k, pl.ds(c, 1), :] for c in range(3)]
+                x = x if a == 0 else x + a * step_x
+                y = y if b == 0 else y + b * step_y
+                parts = pair_sums(rows, (x, y, z, period))
+                total = parts if total is None else [t + p for t, p in zip(total, parts)]
+            for c in range(3):
+                force[n, c, at, :] = total[c]
+            return carry
+
+        lax.fori_loop(0, trips, body, 0)
+
+    def rows_of(number):
+        out = jnp.zeros((slots, slots), f32)
+        for n in range(number):
+            for c in range(3):
+                out = jnp.where(lane == 8 * n + c, jnp.sum(force[n, c], axis=1, keepdims=True), out)
+        return out.T
+
+    dead = [third[wide_slot(a, b), pl.ds(0, 1), :] > 0.1 * far_away for a, b in RING]
+    trips = [
+        (jnp.sum(jnp.where(gone, 0.0, 1.0)).astype(jnp.int32) + (block - 1)) // block for gone in dead
+    ]
+    columns([third[wide_slot(a, b)] for a, b in RING])
+    for n, (a, b) in enumerate(RING):
+        pushes(n, trips[n], [(third, wide_slot(a + p, b + q), p, q) for p, q in RING])
+    push = rows_of(len(RING))
+    speed, place = (tiles[1], tiles[0])
+    for n, (a, b) in enumerate(RING):
+        now = third[wide_slot(a, b)]
+        mine = push[8 * n : 8 * n + 8]
+        kick = jnp.broadcast_to(first[n, pl.ds(3, 1), :], (8, slots))
+        if n == OWN:
+            speed = speed + mine * kick
+            place = place + timestep * speed
+            moved = place * (1.0 / cutoff)
+        else:
+            moved = now + (now - second[n]) + (timestep / cutoff) * (mine * kick)
+        later[n] = jnp.where(jnp.broadcast_to(dead[n], (8, slots)), now, moved)
+    columns([later[OWN]])
+    pushes(0, trips[OWN], [(later, n, a, b) for n, (a, b) in enumerate(RING)])
+    kick = jnp.broadcast_to(first[OWN, pl.ds(3, 1), :], (8, slots))
+    speed = speed + rows_of(1)[:8] * kick
+    place = place + timestep * speed
+    alive = tiles[4] > 0
+    place = jnp.where(alive, place, tiles[2])
+    speed = jnp.where(alive, speed, tiles[3])
     for c in range(3):
         pos_out[c, 0] = place[c : c + 1]
         vel_out[c, 0] = speed[c : c + 1]
@@ -537,14 +608,14 @@
     def in_hbm(x):
         return pltpu.with_memory_space_constraint(x, pltpu.HBM)
 
-    turned, force, own, late, tiles = pl.pallas_call(
+    turned, *states = pl.pallas_call(
         functools.partial(collide_kernel, shape),
         out_shape=[
             pltpu.VMEM(solvent.shape, f32),
-            pltpu.VMEM((3, slots, slots), f32),
-            pltpu.VMEM((3, slots, slots), f32),
-            pltpu.VMEM((3, 8, slots), f32),
-            pltpu.VMEM((6, 8, slots), f32),
+            pltpu.VMEM((9, 8, slots), f32),
+            pltpu.VMEM((9, 8, slots), f32),
+            pltpu.VMEM((25, 8, slots), f32),
+            pltpu.VMEM((5, 8, slots), f32),
         ],
         in_specs=[hbm, smem] + [hbm] * 6,
         out_specs=[vmem] * 5,
@@ -568,15 +639,20 @@
             pltpu.VMEM((2, tall, width_z), f32),
             pltpu.VMEM((2, n_x + 1, 8, width_z), f32),
             pltpu.VMEM((4, 8, width_z), f32),
-            pltpu.VMEM((SUBSTEPS, 9, 8, slots), f32),
+            pltpu.VMEM((2, 9, 8, slots), f32),
+            pltpu.VMEM((25, 8, slots), f32),
+            pltpu.VMEM((3, slots, slots), f32),
+            pltpu.VMEM((3, slots, slots), f32),
             dma((6,)),
             dma((n_x,)),
             dma((8,)),
             dma((8,)),
             dma((3,)),
             dma((3,)),
-            dma((SUBSTEPS, 9)),
-            dma((SUBSTEPS, 9)),
+            dma((2, 9)),
+            dma((2, 9)),
+            dma((25,)),
+            dma((25,)),
         ],
         compiler_params=pltpu.CompilerParams(
             collective_id=0, has_side_effects=True, vmem_limit_bytes=32 * 2**20
@@ -587,7 +663,6 @@
         in_hbm(colloid_pos), in_hbm(colloid_vel), in_hbm(colloid_mass),
     )
 
-    parts = 2
     solvent_out, pos_out, vel_out = pl.pallas_call(
         functools.partial(finish_kernel, shape),
         out_shape=[
@@ -597,11 +672,15 @@
         ],
         in_specs=[vmem] * 5,
         out_specs=[hbm, vmem, vmem],
-        scratch_shapes=[dma((3 * parts,))],
-        input_output_aliases={},
-        compiler_params=pltpu.CompilerParams(vmem_limit_bytes=8 * 2**20),
+        scratch_shapes=[
+            pltpu.VMEM((9, 3, slots, slots), f32),
+            pltpu.VMEM((9, 3, slots, slots), f32),
+            pltpu.VMEM((9, 8, slots), f32),
+            dma((3,)),
+        ],
+        compiler_params=pltpu.CompilerParams(vmem_limit_bytes=16 * 2**20),
         name="finish",
-    )(turned, force, own, late, tiles)
+    )(turned, *states)
     return (solvent_out.reshape(solvent_vel.shape), pos_out, vel_out)
 
 

time: 29.4 us -> 28.1 us (0.956)
  Pallas kernels: 28 us -> 26.7 us
    pallas_call x1, Pallas kernels: 25.7 us -> 22.5 us  [per_device(): pl.pallas_call(functools.partial(collide_kernel, shape), out_shape=[pltpu...]
    pallas_call x1, Pallas kernels: 2.28 us -> 4.11 us  [per_device(): pl.pallas_call(functools.partial(finish_kernel, shape), out_shape=[jax.Sh...]
where the time goes in v3:
time: 28.1 us; the launch traced here: 27.9 us
  Pallas kernels  26.7 us (95%)
  between operations  1.29 us (5%)
    pallas_call x1, Pallas kernels, per_device(): pl.pallas_call(functools.partial(collide_kernel, shape), out_shape=[pltpu...  22.5 us
    pallas_call x1, Pallas kernels, per_device(): pl.pallas_call(functools.partial(finish_kernel, shape), out_shape=[jax.Sh...  4.11 us

profile of v3, /device:TPU:0, one launch (start us, length us, event | category | flops | bytes accessed | tf_op | source)
XLA Modules:
  0.0 27.9 jit_solution(9079788932211929184)
XLA Ops:
  1.3 22.5 %collide.1 = (f32[3,32,64,128]{3,2,1,0:T(8,128)S(1)}, f32[9,8,128]{2,1,0:T(8,128)S(1)}, f32[9,8,128]{2,1,0:T(8,128)S(1)}, f32[25,8,128]{2,1,0:T(8,128)S(1)}, f32[5,8,128]{2,1,0:T(8,128)S(1)}) custom-call(s32[3]{0:T(128)} %shift_hbm.1, s32[1,1]{1,0:T(1,128)S(6)} %copy.11.count, f32[3,32,64,128]{3,2,1,0:T(8,128)} %bitcast.2, s32[32,32,128]{2,1,0:T(8,128)} %occupancy_hbm.1, ...), custom_call_target="tpu_custom_call" | custom-call | tf_op jit(solution)/shard_map/collide/pallas_call | solution.py:611
  23.8 4.1 %finish.1 = (f32[3,32,64,128]{3,2,1,0:T(8,128)}, f32[3,1,1,128]{3,2,1,0:T(1,128)}, f32[3,1,1,128]{3,2,1,0:T(1,128)}) custom-call(f32[3,32,64,128]{3,2,1,0:T(8,128)S(1)} %get-tuple-element.11.turned, f32[9,8,128]{2,1,0:T(8,128)S(1)} %get-tuple-element.12.first, f32[9,8,128]{2,1,0:T(8,128)S(1)} %get-tuple-element.13.second, ...), custom_call_target="tpu_custom_call" | custom-call | tf_op jit(solution)/shard_map/finish/pallas_call | solution.py:666

commit v4 on v3

--- a/solution.py
+++ b/solution.py
@@ -26,7 +26,6 @@
 bf16 = jnp.bfloat16
 RING = [(a, b) for a in (-1, 0, 1) for b in (-1, 0, 1)]
 AROUND = [pair for pair in RING if pair != (0, 0)]
-WIDE = [(a, b) for a in (-1, 1, -2, 2, 0) for b in (-1, 0, 1, -2, 2) if (a, b) != (0, 0)]
 OWN = 4
 
 
@@ -38,8 +37,38 @@
     return (a + 1) * 3 + b + 1
 
 
-def wide_slot(a, b):
-    return (a + 2) * 5 + b + 2
+def folded(b, size_y):
+    return 2 if b == -2 and size_y == 4 else b
+
+
+def wide_slot(a, b, size_y):
+    return (a + 2) * 5 + folded(b, size_y) + 2
+
+
+def wide_pairs(size_y):
+    return [
+        (a, b) for a in (-1, 1, -2, 2, 0) for b in (-1, 0, 1, -2, 2)
+        if (a, b) != (0, 0) and folded(b, size_y) == b
+    ]
+
+
+def sides(me_x):
+    quick = 1 - 2 * (me_x & 1)
+    return (0, quick, -quick)
+
+
+def reader(ref, slot, p, q, steps):
+    period, step_x, step_y = steps
+
+    def read():
+        x, y, z = [ref[slot, pl.ds(c, 1), :] for c in range(3)]
+        if not isinstance(p, int):
+            x = x + p.astype(f32) * step_x
+        elif p != 0:
+            x = x + p * step_x
+        return (x, y if q == 0 else y + q * step_y, z, period)
+
+    return read
 
 
 def terms(value, number):
@@ -105,7 +134,7 @@
 
 
 def force_pass(own, force, sources, first):
-    slots = own.shape[1]
+    slots = own.shape[-1]
     wide = 32 if slots % 32 == 0 else 8
 
     def block(r, carry):
@@ -134,16 +163,22 @@
     return out
 
 
+def flipped(tiles):
+    slots = tiles[0].shape[1]
+    pad = jnp.zeros((slots - 8 * len(tiles), slots), f32)
+    return jnp.concatenate(tiles + [pad], axis=0).T
+
+
 def own_columns(own, tile):
     slots = tile.shape[1]
-    block = jnp.concatenate([tile, jnp.zeros((slots - 8, slots), f32)], axis=0).T
+    block = flipped([tile])
     for c in range(3):
         own[c] = jnp.broadcast_to(block[:, c : c + 1], (slots, slots))
 
 
 def collide_kernel(
     shape, shift_hbm, count, solvent_hbm, occupancy_hbm, axis_hbm, pos_hbm, vel_hbm, mass_hbm,
-    out, first, second, third, tiles,
+    out, first, second, third, tiles, early, begun,
     shift, pos, vel, mass, axis, occupancy, held, cell, sums, total, index, edge_x, edge_y, edge_c,
     normals, fields, halo_x, halo_y, halo_c, src, wide, force, own,
     small_sem, chunk_sem, halo_send, halo_got, edge_send, edge_got, src_send, src_got,
@@ -165,9 +200,10 @@
             device_id=where, device_id_type=MESH,
         )
 
+    around = wide_pairs(size_y)
     edge_c[...] = jnp.zeros_like(edge_c)
     barrier = pltpu.get_barrier_semaphore()
-    for a, b in WIDE:
+    for a, b in around:
         pl.semaphore_signal(barrier, inc=1, device_id=device(a, b), device_id_type=MESH)
 
     small = [
@@ -284,7 +320,7 @@
     finish(n_x - 1)
     finish(n_x)
 
-    pl.semaphore_wait(barrier, len(WIDE))
+    pl.semaphore_wait(barrier, len(around))
 
     def exchange(step):
         mine = src.at[step, OWN, pl.ds(0, 4)]
@@ -330,21 +366,12 @@
     for copy in edges:
         copy.start()
 
-    period = (width_z // 2) / cutoff
-    step_x, step_y = (n_x / cutoff, n_y / cutoff)
-    side = 1 - 2 * (me_x & 1)
-    quick, slow = (side, -side)
+    steps = ((width_z // 2) / cutoff, n_x / cutoff, n_y / cutoff)
+    columns_x = sides(me_x)
+    quick, slow = columns_x[1:]
 
     def source(step, a, b):
-        slot = slot_of(a, b)
-        offset = None if isinstance(a, int) else a.astype(f32) * step_x
-
-        def read():
-            x, y, z = [src[step, slot, pl.ds(c, 1), :] for c in range(3)]
-            x = x if offset is None else x + offset
-            return (x, y if b == 0 else y + b * step_y, z, period)
-
-        return read
+        return reader(src.at[step], slot_of(a, b), a, b, steps)
 
     def arrived(step, a, b):
         slot = slot_of(a, b)
@@ -480,19 +507,30 @@
 
     speed = speed + push * kick
     place_now = place_now + timestep * speed
-    mine = wide_slot(0, 0)
+    def at_wide(a, b):
+        return wide_slot(a, b, size_y)
+
+    mine = at_wide(0, 0)
     wide[mine] = place_now * (1.0 / cutoff)
-    spread = []
-    for a, b in WIDE:
-        k = wide_slot(a, b)
-        spread.append(
+    spread = {}
+    for a, b in around:
+        k, target = (at_wide(a, b), at_wide(-a, -b))
+        spread[a, b] = remote(
+            wide.at[mine, pl.ds(0, 4)], wide.at[target, pl.ds(0, 4)],
+            wide_send.at[k], wide_got.at[target], device(a, b),
+        )
+        spread[a, b].start()
+
+    def wide_arrived(a):
+        for b in (-1, 0, 1, -2, 2):
+            if (isinstance(a, int) and b == 0) or folded(b, size_y) != b:
+                continue
+            k = at_wide(a, b)
             remote(
-                wide.at[mine, pl.ds(0, 4)], wide.at[24 - k, pl.ds(0, 4)],
-                wide_send.at[k], wide_got.at[24 - k], device(a, b),
-            )
-        )
-    for copy in spread:
-        copy.start()
+                wide.at[mine, pl.ds(0, 4)], wide.at[k, pl.ds(0, 4)],
+                wide_send.at[k], wide_got.at[k], device(0, 1),
+            ).wait_recv()
+
     idle_work(2)
     first[...] = src[0]
     second[...] = src[1]
@@ -501,84 +539,126 @@
     tiles[2] = stacked([pos[c, 0] for c in range(3)])
     tiles[3] = stacked([vel[c, 0] for c in range(3)])
     tiles[4] = jnp.broadcast_to(jnp.where(alive, 1.0, 0.0), (8, slots))
-    for copy in spread:
-        copy.wait_recv()
+    for k, a in enumerate(columns_x[:2]):
+        wide_arrived(a)
+        block = flipped([wide[at_wide(a, b)] for b in (-1, 0, 1)])
+        for m in range(3):
+            for c in range(3):
+                column = block[:, 8 * m + c : 8 * m + c + 1]
+                early[3 * k + m, c] = jnp.broadcast_to(column, (slots, slots))
+        for m in range(3):
+            around_m = [reader(wide, at_wide(a, m - 1 + q), a, q, steps) for q in (-1, 0, 1)]
+            force_pass(early.at[m], begun.at[m], around_m, k == 0)
+    wide_arrived(slow)
+    for a in (-2 * quick, 2 * quick):
+        wide_arrived(a)
     third[...] = wide[...]
-    for copy in sends + halo + edges + spread:
+    for copy in sends + halo + edges + list(spread.values()):
         copy.wait_send()
 
 
 def finish_kernel(
-    shape, turned, first, second, third, tiles, out, pos_out, vel_out, own, force, later, sem
+    shape, turned, first, second, third, tiles, early, begun,
+    out, pos_out, vel_out, own, force, later, sums, sem
 ):
     width_x, width_y, width_z = shape
     n_x, n_y = (width_x // SUB, width_y // SUB)
     slots = first.shape[2]
+    size_y = lax.axis_size("yz")
+    columns_x = sides(lax.axis_index("gx"))
     copies = []
     for c in range(3):
         copies.append(pltpu.make_async_copy(turned.at[c], out.at[c], sem.at[c]))
         copies[-1].start()
 
-    period = (width_z // 2) / cutoff
-    step_x, step_y = (n_x / cutoff, n_y / cutoff)
-    lane = iota((slots, slots), 1)
+    steps = ((width_z // 2) / cutoff, n_x / cutoff, n_y / cutoff)
     block = 16 if slots % 16 == 0 else 8
-
-    def columns(group):
-        pad = jnp.zeros((slots - 8 * len(group), slots), f32)
-        flipped = jnp.concatenate(group + [pad], axis=0).T
-        for n in range(len(group)):
-            for c in range(3):
-                own[n, c] = jnp.broadcast_to(flipped[:, 8 * n + c : 8 * n + c + 1], (slots, slots))
-
-    def pushes(n, trips, sources):
+    half = slots // 2
+    group = [(k, b) for k in range(3) for b in (-1, 0, 1)]
+
+    def at_wide(k, b, p=0):
+        return wide_slot(columns_x[k] + p, b, size_y)
+
+    def halves(most, work):
+        work(0)
+        pl.when(most * block > half)(lambda: work(half))
+
+    def columns(tiles, most):
+        sums[...] = flipped(tiles)
+
+        def work(start):
+            at = pl.ds(start, half)
+            for n in range(len(tiles)):
+                for c in range(3):
+                    column = sums[at, 8 * n + c : 8 * n + c + 1]
+                    own[n, c, at, :] = jnp.broadcast_to(column, (half, slots))
+
+        halves(most, work)
+
+    def pushes(m, columns_of, trips, sources, before=None):
         def body(r, carry):
             at = pl.ds(pl.multiple_of(r * block, block), block)
-            rows = [own[n, c, at, :] for c in range(3)]
-            total = None
-            for ref, k, a, b in sources:
-                x, y, z = [ref[k, pl.ds(c, 1), :] for c in range(3)]
-                x = x if a == 0 else x + a * step_x
-                y = y if b == 0 else y + b * step_y
-                parts = pair_sums(rows, (x, y, z, period))
+            rows = [columns_of[c, at, :] for c in range(3)]
+            total = None if before is None else [before[c, at, :] for c in range(3)]
+            for source in sources:
+                parts = pair_sums(rows, source())
                 total = parts if total is None else [t + p for t, p in zip(total, parts)]
             for c in range(3):
-                force[n, c, at, :] = total[c]
+                force[m, c, at, :] = total[c]
             return carry
 
         lax.fori_loop(0, trips, body, 0)
 
-    def rows_of(number):
-        out = jnp.zeros((slots, slots), f32)
-        for n in range(number):
-            for c in range(3):
-                out = jnp.where(lane == 8 * n + c, jnp.sum(force[n, c], axis=1, keepdims=True), out)
-        return out.T
-
-    dead = [third[wide_slot(a, b), pl.ds(0, 1), :] > 0.1 * far_away for a, b in RING]
+    def rows_of(number, most):
+        lane = iota((half, slots), 1)
+
+        def work(start):
+            at = pl.ds(start, half)
+            block = jnp.zeros((half, slots), f32)
+            for n in range(number):
+                for c in range(3):
+                    total = jnp.sum(force[n, c, at, :], axis=1, keepdims=True)
+                    block = jnp.where(lane == 8 * n + c, total, block)
+            sums[at, :] = block
+
+        halves(most, work)
+        return sums[...].T
+
+    dead = [third[at_wide(k, b), pl.ds(0, 1), :] > 0.1 * far_away for k, b in group]
     trips = [
         (jnp.sum(jnp.where(gone, 0.0, 1.0)).astype(jnp.int32) + (block - 1)) // block for gone in dead
     ]
-    columns([third[wide_slot(a, b)] for a, b in RING])
-    for n, (a, b) in enumerate(RING):
-        pushes(n, trips[n], [(third, wide_slot(a + p, b + q), p, q) for p, q in RING])
-    push = rows_of(len(RING))
+    most = functools.reduce(jnp.maximum, trips)
+    columns([third[at_wide(2, b)] for b in (-1, 0, 1)], most)
+    for m, (k, b) in enumerate(group):
+        if k == 0:
+            slow = columns_x[2]
+            around_m = [reader(third, at_wide(2, b + q), slow, q, steps) for q in (-1, 0, 1)]
+            pushes(m, early.at[m], trips[m], around_m, begun.at[m])
+        else:
+            around_m = [
+                reader(third, at_wide(k, b + q, p), p, q, steps) for p in (-1, 0, 1) for q in (-1, 0, 1)
+            ]
+            pushes(m, early.at[m] if k == 1 else own.at[m - 6], trips[m], around_m)
+    push = rows_of(len(group), most)
     speed, place = (tiles[1], tiles[0])
-    for n, (a, b) in enumerate(RING):
-        now = third[wide_slot(a, b)]
-        mine = push[8 * n : 8 * n + 8]
-        kick = jnp.broadcast_to(first[n, pl.ds(3, 1), :], (8, slots))
-        if n == OWN:
+    for m, (k, b) in enumerate(group):
+        near = slot_of(columns_x[k], b)
+        now = third[at_wide(k, b)]
+        mine = push[8 * m : 8 * m + 8]
+        kick = jnp.broadcast_to(first[near, pl.ds(3, 1), :], (8, slots))
+        if (k, b) == (0, 0):
             speed = speed + mine * kick
             place = place + timestep * speed
             moved = place * (1.0 / cutoff)
+            own_kick, own_trips = (kick, trips[m])
         else:
-            moved = now + (now - second[n]) + (timestep / cutoff) * (mine * kick)
-        later[n] = jnp.where(jnp.broadcast_to(dead[n], (8, slots)), now, moved)
-    columns([later[OWN]])
-    pushes(0, trips[OWN], [(later, n, a, b) for n, (a, b) in enumerate(RING)])
-    kick = jnp.broadcast_to(first[OWN, pl.ds(3, 1), :], (8, slots))
-    speed = speed + rows_of(1)[:8] * kick
+            moved = now + (now - second[near]) + (timestep / cutoff) * (mine * kick)
+        later[m] = jnp.where(jnp.broadcast_to(dead[m], (8, slots)), now, moved)
+    columns([later[1]], own_trips)
+    around_m = [reader(later, m, columns_x[k], b, steps) for m, (k, b) in enumerate(group)]
+    pushes(0, own.at[0], own_trips, around_m)
+    speed = speed + rows_of(1, own_trips)[:8] * own_kick
     place = place + timestep * speed
     alive = tiles[4] > 0
     place = jnp.where(alive, place, tiles[2])
@@ -616,9 +696,11 @@
             pltpu.VMEM((9, 8, slots), f32),
             pltpu.VMEM((25, 8, slots), f32),
             pltpu.VMEM((5, 8, slots), f32),
+            pltpu.VMEM((6, 3, slots, slots), f32),
+            pltpu.VMEM((3, 3, slots, slots), f32),
         ],
         in_specs=[hbm, smem] + [hbm] * 6,
-        out_specs=[vmem] * 5,
+        out_specs=[vmem] * 7,
         scratch_shapes=[
             pltpu.SMEM(grid_shift.shape, jnp.int32),
             pltpu.VMEM(colloid_pos.shape, f32),
@@ -670,12 +752,13 @@
             jax.ShapeDtypeStruct(colloid_pos.shape, f32),
             jax.ShapeDtypeStruct(colloid_vel.shape, f32),
         ],
-        in_specs=[vmem] * 5,
+        in_specs=[vmem] * 7,
         out_specs=[hbm, vmem, vmem],
         scratch_shapes=[
-            pltpu.VMEM((9, 3, slots, slots), f32),
+            pltpu.VMEM((3, 3, slots, slots), f32),
             pltpu.VMEM((9, 3, slots, slots), f32),
             pltpu.VMEM((9, 8, slots), f32),
+            pltpu.VMEM((slots, slots), f32),
             dma((3,)),
         ],
         compiler_params=pltpu.CompilerParams(vmem_limit_bytes=16 * 2**20),

time: 28.1 us -> 27.5 us (0.979); the launches traced: 27.9 us -> 27.9 us
  no operation moved by 1% of the time
where the time goes in v4:
time: 27.5 us; the launch traced here: 27.9 us
  Pallas kernels  26.6 us (97%)
  between operations  1.29 us (5%)
    pallas_call x1, Pallas kernels, per_device(): pl.pallas_call(functools.partial(collide_kernel, shape), out_shape=[pltpu...  22.5 us
    pallas_call x1, Pallas kernels, per_device(): pl.pallas_call(functools.partial(finish_kernel, shape), out_shape=[jax.Sh...  4.08 us

profile of v4, /device:TPU:0, one launch (start us, length us, event | category | flops | bytes accessed | tf_op | source)
XLA Modules:
  0.0 27.9 jit_solution(2700887022333715209)
XLA Ops:
  1.3 22.5 %collide.1 = (f32[3,32,64,128]{3,2,1,0:T(8,128)S(1)}, f32[9,8,128]{2,1,0:T(8,128)S(1)}, f32[9,8,128]{2,1,0:T(8,128)S(1)}, f32[25,8,128]{2,1,0:T(8,128)S(1)}, f32...) custom-call(s32[3]{0:T(128)} %shift_hbm.1, s32[1,1]{1,0:T(1,128)S(6)} %copy.11.count, ...), custom_call_target="tpu_custom_call" | custom-call | tf_op jit(solution)/shard_map/collide/pallas_call | solution.py:691
  23.8 4.1 %finish.1 = (f32[3,32,64,128]{3,2,1,0:T(8,128)}, f32[3,1,1,128]{3,2,1,0:T(1,128)}, f32[3,1,1,128]{3,2,1,0:T(1,128)}) custom-call(f32[3,32,64,128]{3,2,1,0:T(8,128)S(1)} %get-tuple-element.13.turned, f32[9,8,128]{2,1,0:T(8,128)S(1)} %get-tuple-element.14.first, f32[9,8,128]{2,1,0:T(8,128)S(1)} %get-tuple-element.15.second, ...), custom_call_target="tpu_custom_call" | custom-call | tf_op jit(solution)/shard_map/finish/pallas_call | solution.py:748

commit v5 on v4

--- a/solution.py
+++ b/solution.py
@@ -202,10 +202,6 @@
 
     around = wide_pairs(size_y)
     edge_c[...] = jnp.zeros_like(edge_c)
-    barrier = pltpu.get_barrier_semaphore()
-    for a, b in around:
-        pl.semaphore_signal(barrier, inc=1, device_id=device(a, b), device_id_type=MESH)
-
     small = [
         pltpu.make_async_copy(source, target, small_sem.at[k])
         for k, (source, target) in enumerate(
@@ -221,8 +217,18 @@
         )
         for i in range(n_x)
     ]
-    for copy in small + chunks:
+    barrier = pltpu.get_barrier_semaphore()
+
+    def greet(pairs):
+        for a, b in pairs:
+            pl.semaphore_signal(barrier, inc=1, device_id=device(a, b), device_id_type=MESH)
+
+    for copy in small:
         copy.start()
+    greet(around[:6])
+    for copy in chunks:
+        copy.start()
+    greet(around[6:])
     for copy in small[:-1]:
         copy.wait()
     shift_x, shift_y, shift_z = (shift[0], shift[1], shift[2])

time: 27.5 us -> 26.5 us (0.964); the launches traced: 27.9 us -> 26.5 us
  Pallas kernels: 26.6 us -> 25.2 us
    pallas_call x1, Pallas kernels: 4.08 us -> 3.35 us  [per_device(): pl.pallas_call(functools.partial(finish_kernel, shape), out_shape=[jax.Sh...]
    pallas_call x1, Pallas kernels: 22.5 us -> 21.9 us  [per_device(): pl.pallas_call(functools.partial(collide_kernel, shape), out_shape=[pltpu...]
where the time goes in v5:
time: 26.5 us
  Pallas kernels  25.2 us (95%)
  between operations  1.29 us (5%)
    pallas_call x1, Pallas kernels, per_device(): pl.pallas_call(functools.partial(collide_kernel, shape), out_shape=[pltpu...  21.9 us
    pallas_call x1, Pallas kernels, per_device(): pl.pallas_call(functools.partial(finish_kernel, shape), out_shape=[jax.Sh...  3.35 us

profile of v5, /device:TPU:0, one launch (start us, length us, event | category | flops | bytes accessed | tf_op | source)
XLA Modules:
  0.0 26.5 jit_solution(4714796161291705567)
XLA Ops:
  1.3 21.9 %collide.1 = (f32[3,32,64,128]{3,2,1,0:T(8,128)S(1)}, f32[9,8,128]{2,1,0:T(8,128)S(1)}, f32[9,8,128]{2,1,0:T(8,128)S(1)}, f32[25,8,128]{2,1,0:T(8,128)S(1)}, f32...) custom-call(s32[3]{0:T(128)} %shift_hbm.1, s32[1,1]{1,0:T(1,128)S(6)} %copy.11.count, ...), custom_call_target="tpu_custom_call" | custom-call | tf_op jit(solution)/shard_map/collide/pallas_call | solution.py:697
  23.1 3.4 %finish.1 = (f32[3,32,64,128]{3,2,1,0:T(8,128)}, f32[3,1,1,128]{3,2,1,0:T(1,128)}, f32[3,1,1,128]{3,2,1,0:T(1,128)}) custom-call(f32[3,32,64,128]{3,2,1,0:T(8,128)S(1)} %get-tuple-element.13.turned, f32[9,8,128]{2,1,0:T(8,128)S(1)} %get-tuple-element.14.first, f32[9,8,128]{2,1,0:T(8,128)S(1)} %get-tuple-element.15.second, ...), custom_call_target="tpu_custom_call" | custom-call | tf_op jit(solution)/shard_map/finish/pallas_call | solution.py:754

commit v6 on v5

--- a/solution.py
+++ b/solution.py
@@ -133,12 +133,12 @@
     return [weight * dx, weight * dy, weight * dz]
 
 
-def force_pass(own, force, sources, first):
+def force_pass(own, force, sources, first, straight=False):
     slots = own.shape[-1]
     wide = 32 if slots % 32 == 0 else 8
 
     def block(r, carry):
-        at = pl.ds(pl.multiple_of(r * wide, wide), wide)
+        at = pl.ds(r * wide if straight else pl.multiple_of(r * wide, wide), wide)
         rows = [own[c, at, :] for c in range(3)]
         total = None if first else [force[c, at, :] for c in range(3)]
         for source in sources:
@@ -148,7 +148,11 @@
             force[c, at, :] = total[c]
         return carry
 
-    lax.fori_loop(0, slots // wide, block, 0)
+    if straight:
+        for r in range(slots // wide):
+            block(r, 0)
+    else:
+        lax.fori_loop(0, slots // wide, block, 0)
 
 
 def force_rows(force):
@@ -180,7 +184,7 @@
     shape, shift_hbm, count, solvent_hbm, occupancy_hbm, axis_hbm, pos_hbm, vel_hbm, mass_hbm,
     out, first, second, third, tiles, early, begun,
     shift, pos, vel, mass, axis, occupancy, held, cell, sums, total, index, edge_x, edge_y, edge_c,
-    normals, fields, halo_x, halo_y, halo_c, src, wide, force, own,
+    normals, fields, halo_x, halo_y, halo_c, src, wide, force, own, table,
     small_sem, chunk_sem, halo_send, halo_got, edge_send, edge_got, src_send, src_got,
     wide_send, wide_got,
 ):
@@ -268,6 +272,8 @@
     number = axis[...].reshape(n_x * n_y, width_z // 2).astype(f32).astype(bf16)
     index[...] = dot(number, expand).reshape(n_x, n_y, width_z)
 
+    for c, part in enumerate(axes_of(iota((DIRECTIONS, slots), 0).astype(f32))):
+        table[c] = part
     start = stacked([jnp.where(alive, pos[0, 0], far_away), pos[1, 0], pos[2, 0]])
     kick = jnp.broadcast_to((timestep * stiffness * cutoff) / mass[0], (8, slots))
     src[0, OWN] = jnp.where(comp == 3, kick, start * (1.0 / cutoff))
@@ -399,16 +405,16 @@
             arrived(step, slow, b)
 
     def late_forces(step):
-        late_arrivals(step)
-        force_pass(own, force, [source(step, slow, b) for b in (-1, 0, 1)], False)
+        force_pass(own, force, [source(step, slow, b) for b in (-1, 0, 1)], False, True)
         return force_rows(force)
 
     own_columns(own, src[0, OWN])
     early_forces(0)
+    late_arrivals(0)
+    for copy in edges + halo:
+        copy.wait_recv()
     push = late_forces(0)
 
-    for copy in halo:
-        copy.wait_recv()
     total[...] = sums[...]
     total[0] += halo_x[0]
     total[n_x] += halo_x[1]
@@ -419,8 +425,6 @@
     total[0, at_high, :] += halo_c[1, at_low, :]
     total[n_x, at_low, :] += halo_c[2, at_low, :]
     total[n_x, at_high, :] += halo_c[3, at_low, :]
-    for copy in edges:
-        copy.wait_recv()
 
     chosen = (iota((width_z, slots), 0) == layer_z).astype(f32).astype(bf16)
     block = total[...].reshape((n_x + 1) * tiles_y * 8, width_z)
@@ -441,10 +445,16 @@
     found = jnp.zeros((8, slots), f32)
     for n, mask in enumerate(wanted):
         found = found + jnp.where(mask, at_z[8 * n : 8 * n + 8], 0.0)
-    found = jnp.sum(found, axis=0, keepdims=True)
+    name = jnp.sum(found, axis=0, keepdims=True).astype(jnp.int32)
     heavy = jnp.maximum(picked[3:4], fill_mass)
     mean = [picked[c : c + 1] / heavy for c in range(3)]
-    n = axes_of(found)
+    n = []
+    for c in range(3):
+        hit = [
+            jnp.where(iota((8, slots), 0) + 8 * r == name, table[c, pl.ds(8 * r, 8), :], 0.0)
+            for r in range(DIRECTIONS // 8)
+        ]
+        n.append(jnp.sum(sum(hit), axis=0, keepdims=True))
     rel = [vel[c, 0] - mean[c] for c in range(3)]
     cross = [n[1] * rel[2] - n[2] * rel[1], n[2] * rel[0] - n[0] * rel[2], n[0] * rel[1] - n[1] * rel[0]]
     along = n[0] * rel[0] + n[1] * rel[1] + n[2] * rel[2]
@@ -509,6 +519,7 @@
     own_columns(own, src[1, OWN])
     idle_work(1)
     early_forces(1)
+    late_arrivals(1)
     push = late_forces(1)
 
     speed = speed + push * kick
@@ -731,6 +742,7 @@
             pltpu.VMEM((25, 8, slots), f32),
             pltpu.VMEM((3, slots, slots), f32),
             pltpu.VMEM((3, slots, slots), f32),
+            pltpu.VMEM((3, DIRECTIONS, slots), f32),
             dma((6,)),
             dma((n_x,)),
             dma((8,)),

time: 26.5 us -> 26.5 us (level); the launches traced: 26.5 us -> 26.2 us
  Pallas kernels: 25.2 us -> 24.9 us
where the time goes in v6:
time: 26.5 us; the launch traced here: 26.2 us
  Pallas kernels  24.9 us (94%)
  between operations  1.29 us (5%)
    pallas_call x1, Pallas kernels, per_device(): pl.pallas_call(functools.partial(collide_kernel, shape), out_shape=[pltpu...  21.6 us
    pallas_call x1, Pallas kernels, per_device(): pl.pallas_call(functools.partial(finish_kernel, shape), out_shape=[jax.Sh...  3.3 us

profile of v6, /device:TPU:0, one launch (start us, length us, event | category | flops | bytes accessed | tf_op | source)
XLA Modules:
  0.0 26.2 jit_solution(3044825043933681539)
XLA Ops:
  1.3 21.6 %collide.1 = (f32[3,32,64,128]{3,2,1,0:T(8,128)S(1)}, f32[9,8,128]{2,1,0:T(8,128)S(1)}, f32[9,8,128]{2,1,0:T(8,128)S(1)}, f32[25,8,128]{2,1,0:T(8,128)S(1)}, f32...) custom-call(s32[3]{0:T(128)} %shift_hbm.1, s32[1,1]{1,0:T(1,128)S(6)} %copy.11.count, ...), custom_call_target="tpu_custom_call" | custom-call | tf_op jit(solution)/shard_map/collide/pallas_call | solution.py:708
  22.9 3.3 %finish.1 = (f32[3,32,64,128]{3,2,1,0:T(8,128)}, f32[3,1,1,128]{3,2,1,0:T(1,128)}, f32[3,1,1,128]{3,2,1,0:T(1,128)}) custom-call(f32[3,32,64,128]{3,2,1,0:T(8,128)S(1)} %get-tuple-element.13.turned, f32[9,8,128]{2,1,0:T(8,128)S(1)} %get-tuple-element.14.first, f32[9,8,128]{2,1,0:T(8,128)S(1)} %get-tuple-element.15.second, ...), custom_call_target="tpu_custom_call" | custom-call | tf_op jit(solution)/shard_map/finish/pallas_call | solution.py:766

commit v7 on v6

--- a/solution.py
+++ b/solution.py
@@ -576,7 +576,7 @@
 
 def finish_kernel(
     shape, turned, first, second, third, tiles, early, begun,
-    out, pos_out, vel_out, own, force, later, sums, sem
+    out, pos_out, vel_out, own, force, later, sums, placed, packed, counts, sem
 ):
     width_x, width_y, width_z = shape
     n_x, n_y = (width_x // SUB, width_y // SUB)
@@ -612,10 +612,12 @@
 
         halves(most, work)
 
-    def pushes(m, columns_of, trips, sources, before=None):
+    def pushes(m, columns_of, trips, sources, before=None, moved=None):
         def body(r, carry):
             at = pl.ds(pl.multiple_of(r * block, block), block)
             rows = [columns_of[c, at, :] for c in range(3)]
+            if moved is not None:
+                rows = [rows[0] + moved[0], rows[1] + moved[1], rows[2]]
             total = None if before is None else [before[c, at, :] for c in range(3)]
             for source in sources:
                 parts = pair_sums(rows, source())
@@ -641,10 +643,46 @@
         halves(most, work)
         return sums[...].T
 
+    comp = iota((8, slots), 0)
+    for a in range(-2, 3):
+        for b in range(-2, 3):
+            tile = third[wide_slot(a, b, size_y)]
+            offset = jnp.where(comp == 0, a * steps[1], jnp.where(comp == 1, b * steps[2], 0.0))
+            placed[(a + 2) * 5 + b + 2] = tile + offset
+            live = jnp.where(tile[:1] > 0.1 * far_away, 0.0, 1.0)
+            counts[(a + 2) * 5 + b + 2] = jnp.sum(live).astype(jnp.int32)
+
+    def at_placed(k, b, p=0):
+        return (columns_x[k] + p + 2) * 5 + b + 2
+
     dead = [third[at_wide(k, b), pl.ds(0, 1), :] > 0.1 * far_away for k, b in group]
-    trips = [
-        (jnp.sum(jnp.where(gone, 0.0, 1.0)).astype(jnp.int32) + (block - 1)) // block for gone in dead
-    ]
+    trips = [(counts[at_placed(k, b)] + (block - 1)) // block for k, b in group]
+    lane_of = iota((8, slots), 1)
+
+    def pack(n, k, b):
+        at = [at_placed(k, b + q, p) for p, q in RING]
+        held = [counts[t] for t in at]
+        best, which, single = (held[0], 0, at[0])
+        for t in range(1, 9):
+            larger = held[t] > best
+            best = jnp.where(larger, held[t], best)
+            which = jnp.where(larger, t, which)
+            single = jnp.where(larger, at[t], single)
+        for t in range(8):
+            held[t] = jnp.where(which == t, held[8], held[t])
+            at[t] = jnp.where(which == t, at[8], at[t])
+        fits = None
+        for t in range(4):
+            size = held[2 * t]
+            both = jnp.where(
+                lane_of < size, placed[at[2 * t]], pltpu.roll(placed[at[2 * t + 1]], size, 1)
+            )
+            packed[4 * n + t] = both
+            fit = size + held[2 * t + 1] <= slots
+            fits = fit if fits is None else jnp.logical_and(fits, fit)
+        return fits, single
+
+    packs = [pack(n, k, b) for n, (k, b) in enumerate(group[3:])]
     most = functools.reduce(jnp.maximum, trips)
     columns([third[at_wide(2, b)] for b in (-1, 0, 1)], most)
     for m, (k, b) in enumerate(group):
@@ -656,7 +694,13 @@
             around_m = [
                 reader(third, at_wide(k, b + q, p), p, q, steps) for p in (-1, 0, 1) for q in (-1, 0, 1)
             ]
-            pushes(m, early.at[m] if k == 1 else own.at[m - 6], trips[m], around_m)
+            own_m = early.at[m] if k == 1 else own.at[m - 6]
+            fits, single = packs[m - 3]
+            tight = [reader(packed, 4 * (m - 3) + t, 0, 0, steps) for t in range(4)]
+            tight.append(reader(placed, single, 0, 0, steps))
+            moved = (columns_x[k].astype(f32) * steps[1], b * steps[2])
+            pushes(m, own_m, jnp.where(fits, trips[m], 0), tight, None, moved)
+            pushes(m, own_m, jnp.where(fits, 0, trips[m]), around_m)
     push = rows_of(len(group), most)
     speed, place = (tiles[1], tiles[0])
     for m, (k, b) in enumerate(group):
@@ -777,6 +821,9 @@
             pltpu.VMEM((9, 3, slots, slots), f32),
             pltpu.VMEM((9, 8, slots), f32),
             pltpu.VMEM((slots, slots), f32),
+            pltpu.VMEM((25, 8, slots), f32),
+            pltpu.VMEM((24, 8, slots), f32),
+            pltpu.SMEM((25,), jnp.int32),
             dma((3,)),
         ],
         compiler_params=pltpu.CompilerParams(vmem_limit_bytes=16 * 2**20),

time: 26.5 us -> 26.5 us (level); the launches traced: 26.2 us -> 26.6 us
  Pallas kernels: 24.9 us -> 25.3 us
    pallas_call x1, Pallas kernels: 3.3 us -> 3.67 us  [per_device(): pl.pallas_call(functools.partial(finish_kernel, shape), out_shape=[jax.Sh...]
where the time goes in v7:
time: 26.5 us; the launch traced here: 26.6 us
  Pallas kernels  25.3 us (95%)
  between operations  1.29 us (5%)
    pallas_call x1, Pallas kernels, per_device(): pl.pallas_call(functools.partial(collide_kernel, shape), out_shape=[pltpu...  21.6 us
    pallas_call x1, Pallas kernels, per_device(): pl.pallas_call(functools.partial(finish_kernel, shape), out_shape=[jax.Sh...  3.67 us

profile of v7, /device:TPU:0, one launch (start us, length us, event | category | flops | bytes accessed | tf_op | source)
XLA Modules:
  0.0 26.6 jit_solution(17461950177642276013)
XLA Ops:
  1.3 21.6 %collide.1 = (f32[3,32,64,128]{3,2,1,0:T(8,128)S(1)}, f32[9,8,128]{2,1,0:T(8,128)S(1)}, f32[9,8,128]{2,1,0:T(8,128)S(1)}, f32[25,8,128]{2,1,0:T(8,128)S(1)}, f32...) custom-call(s32[3]{0:T(128)} %shift_hbm.1, s32[1,1]{1,0:T(1,128)S(6)} %copy.11.count, ...), custom_call_target="tpu_custom_call" | custom-call | tf_op jit(solution)/shard_map/collide/pallas_call | solution.py:752
  22.9 3.7 %finish.1 = (f32[3,32,64,128]{3,2,1,0:T(8,128)}, f32[3,1,1,128]{3,2,1,0:T(1,128)}, f32[3,1,1,128]{3,2,1,0:T(1,128)}) custom-call(f32[3,32,64,128]{3,2,1,0:T(8,128)S(1)} %get-tuple-element.13.turned, f32[9,8,128]{2,1,0:T(8,128)S(1)} %get-tuple-element.14.first, f32[9,8,128]{2,1,0:T(8,128)S(1)} %get-tuple-element.15.second, ...), custom_call_target="tpu_custom_call" | custom-call | tf_op jit(solution)/shard_map/finish/pallas_call | solution.py:810

commit v8 on v7

--- a/solution.py
+++ b/solution.py
@@ -556,6 +556,8 @@
     tiles[2] = stacked([pos[c, 0] for c in range(3)])
     tiles[3] = stacked([vel[c, 0] for c in range(3)])
     tiles[4] = jnp.broadcast_to(jnp.where(alive, 1.0, 0.0), (8, slots))
+    for copy in sends + halo + edges:
+        copy.wait_send()
     for k, a in enumerate(columns_x[:2]):
         wide_arrived(a)
         block = flipped([wide[at_wide(a, b)] for b in (-1, 0, 1)])
@@ -570,7 +572,7 @@
     for a in (-2 * quick, 2 * quick):
         wide_arrived(a)
     third[...] = wide[...]
-    for copy in sends + halo + edges + list(spread.values()):
+    for copy in spread.values():
         copy.wait_send()
 
 
@@ -628,19 +630,20 @@
 
         lax.fori_loop(0, trips, body, 0)
 
-    def rows_of(number, most):
+    def rows_of(trips):
         lane = iota((half, slots), 1)
 
-        def work(start):
+        def work(start, group, block):
             at = pl.ds(start, half)
-            block = jnp.zeros((half, slots), f32)
-            for n in range(number):
+            for n in group:
                 for c in range(3):
                     total = jnp.sum(force[n, c, at, :], axis=1, keepdims=True)
                     block = jnp.where(lane == 8 * n + c, total, block)
             sums[at, :] = block
 
-        halves(most, work)
+        work(0, range(len(trips)), jnp.zeros((half, slots), f32))
+        for n, number in enumerate(trips):
+            pl.when(number * block > half)(lambda n=n: work(half, [n], sums[pl.ds(half, half), :]))
         return sums[...].T
 
     comp = iota((8, slots), 0)
@@ -701,7 +704,7 @@
             moved = (columns_x[k].astype(f32) * steps[1], b * steps[2])
             pushes(m, own_m, jnp.where(fits, trips[m], 0), tight, None, moved)
             pushes(m, own_m, jnp.where(fits, 0, trips[m]), around_m)
-    push = rows_of(len(group), most)
+    push = rows_of(trips)
     speed, place = (tiles[1], tiles[0])
     for m, (k, b) in enumerate(group):
         near = slot_of(columns_x[k], b)
@@ -719,7 +722,7 @@
     columns([later[1]], own_trips)
     around_m = [reader(later, m, columns_x[k], b, steps) for m, (k, b) in enumerate(group)]
     pushes(0, own.at[0], own_trips, around_m)
-    speed = speed + rows_of(1, own_trips)[:8] * own_kick
+    speed = speed + rows_of([own_trips])[:8] * own_kick
     place = place + timestep * speed
     alive = tiles[4] > 0
     place = jnp.where(alive, place, tiles[2])

time: 26.5 us -> 26.5 us (level); the launches traced: 26.6 us -> 26.1 us
  Pallas kernels: 25.3 us -> 24.8 us
    pallas_call x1, Pallas kernels: 3.67 us -> 3.2 us  [per_device(): pl.pallas_call(functools.partial(finish_kernel, shape), out_shape=[jax.Sh...]
where the time goes in v8:
time: 26.5 us; the launch traced here: 26.1 us
  Pallas kernels  24.8 us (94%)
  between operations  1.29 us (5%)
    pallas_call x1, Pallas kernels, per_device(): pl.pallas_call(functools.partial(collide_kernel, shape), out_shape=[pltpu...  21.6 us
    pallas_call x1, Pallas kernels, per_device(): pl.pallas_call(functools.partial(finish_kernel, shape), out_shape=[jax.Sh...  3.2 us

profile of v8, /device:TPU:0, one launch (start us, length us, event | category | flops | bytes accessed | tf_op | source)
XLA Modules:
  0.0 26.1 jit_solution(15312614586673296685)
XLA Ops:
  1.3 21.6 %collide.1 = (f32[3,32,64,128]{3,2,1,0:T(8,128)S(1)}, f32[9,8,128]{2,1,0:T(8,128)S(1)}, f32[9,8,128]{2,1,0:T(8,128)S(1)}, f32[25,8,128]{2,1,0:T(8,128)S(1)}, f32...) custom-call(s32[3]{0:T(128)} %shift_hbm.1, s32[1,1]{1,0:T(1,128)S(6)} %copy.11.count, ...), custom_call_target="tpu_custom_call" | custom-call | tf_op jit(solution)/shard_map/collide/pallas_call | solution.py:755
  22.9 3.2 %finish.1 = (f32[3,32,64,128]{3,2,1,0:T(8,128)}, f32[3,1,1,128]{3,2,1,0:T(1,128)}, f32[3,1,1,128]{3,2,1,0:T(1,128)}) custom-call(f32[3,32,64,128]{3,2,1,0:T(8,128)S(1)} %get-tuple-element.13.turned, f32[9,8,128]{2,1,0:T(8,128)S(1)} %get-tuple-element.14.first, f32[9,8,128]{2,1,0:T(8,128)S(1)} %get-tuple-element.15.second, ...), custom_call_target="tpu_custom_call" | custom-call | tf_op jit(solution)/shard_map/finish/pallas_call | solution.py:813

commit v9 on v8

--- a/solution.py
+++ b/solution.py
@@ -47,7 +47,7 @@
 
 def wide_pairs(size_y):
     return [
-        (a, b) for a in (-1, 1, -2, 2, 0) for b in (-1, 0, 1, -2, 2)
+        (a, b) for a in (-1, 1, -2, 2, 0) for b in (2, -2, 0, -1, 1)
         if (a, b) != (0, 0) and folded(b, size_y) == b
     ]
 
@@ -229,10 +229,10 @@
 
     for copy in small:
         copy.start()
-    greet(around[:6])
+    greet(around[:8])
     for copy in chunks:
         copy.start()
-    greet(around[6:])
+    greet(around[8:])
     for copy in small[:-1]:
         copy.wait()
     shift_x, shift_y, shift_z = (shift[0], shift[1], shift[2])

time: 26.5 us -> 26.5 us (level)
  no operation moved by 1% of the time
where the time goes in v9:
time: 26.5 us; the launch traced here: 26.1 us
  Pallas kernels  24.8 us (94%)
  between operations  1.29 us (5%)
    pallas_call x1, Pallas kernels, per_device(): pl.pallas_call(functools.partial(collide_kernel, shape), out_shape=[pltpu...  21.5 us
    pallas_call x1, Pallas kernels, per_device(): pl.pallas_call(functools.partial(finish_kernel, shape), out_shape=[jax.Sh...  3.26 us

profile of v9, /device:TPU:0, one launch (start us, length us, event | category | flops | bytes accessed | tf_op | source)
XLA Modules:
  0.0 26.1 jit_solution(8993030010793520428)
XLA Ops:
  1.3 21.5 %collide.1 = (f32[3,32,64,128]{3,2,1,0:T(8,128)S(1)}, f32[9,8,128]{2,1,0:T(8,128)S(1)}, f32[9,8,128]{2,1,0:T(8,128)S(1)}, f32[25,8,128]{2,1,0:T(8,128)S(1)}, f32...) custom-call(s32[3]{0:T(128)} %shift_hbm.1, s32[1,1]{1,0:T(1,128)S(6)} %copy.11.count, ...), custom_call_target="tpu_custom_call" | custom-call | tf_op jit(solution)/shard_map/collide/pallas_call | solution.py:755
  22.8 3.3 %finish.1 = (f32[3,32,64,128]{3,2,1,0:T(8,128)}, f32[3,1,1,128]{3,2,1,0:T(1,128)}, f32[3,1,1,128]{3,2,1,0:T(1,128)}) custom-call(f32[3,32,64,128]{3,2,1,0:T(8,128)S(1)} %get-tuple-element.13.turned, f32[9,8,128]{2,1,0:T(8,128)S(1)} %get-tuple-element.14.first, f32[9,8,128]{2,1,0:T(8,128)S(1)} %get-tuple-element.15.second, ...), custom_call_target="tpu_custom_call" | custom-call | tf_op jit(solution)/shard_map/finish/pallas_call | solution.py:813
